TPU v7x, 8 devices: a whole 2x2x1 slice. The times are simulated.
8 devices in a mesh: part: 1 (over z), data: 2 (over y), model: 4 (over x, core).
Axes of the slice: x: 2, y: 2, z: 1, core: 2. Of those that a mesh axis runs over, the one named last changes fastest.
Arguments:
- x_seq: bfloat16 [8, 128, 2048], P(('part', 'data'))
- gy_seq: bfloat16 [8, 128, 2048], P(('part', 'data'), None, 'model')
- h_init: float32 [2, 8, 2048], P(None, ('part', 'data'), 'model')
- c_init: float32 [2, 8, 2048], P(None, ('part', 'data'), 'model')
- w_in: bfloat16 [2048, 4, 2048], P(None, None, 'model')
- w_up: bfloat16 [1, 2048, 4, 2048], P(None, None, None, 'model')
- w_rec: bfloat16 [2, 2048, 4, 2048], P(None, None, None, 'model')
- gate_bias: float32 [2, 4, 2048], P(None, None, 'model')
Outputs:
- output 1: bfloat16 [8, 128, 2048], P(('part', 'data'), None, 'model')
- output 2: float32 [2, 8, 2048], P(None, ('part', 'data'), 'model')
- output 3: float32 [2, 8, 2048], P(None, ('part', 'data'), 'model')
- output 4: float32 [2048, 4, 2048], P('part', None, 'model')
- output 5: float32 [1, 2048, 4, 2048], P(None, 'part', None, 'model')
- output 6: float32 [2, 2048, 4, 2048], P(None, 'part', None, 'model')
- output 7: float32 [2, 4, 2048], P(None, 'part', 'model')
All inputs are finite; a program needn't handle non-finite values.
Results may differ from a plain program's by a relative error of at most 0.012509.
Values are sent between devices in bfloat16 or wider.
A program may use at most 1 GiB of HBM per device.

v0:
```python
import jax
import jax.numpy as jnp
from jax import lax
from jax.sharding import PartitionSpec as P


def lstm_cell(gate_pre, c_prev):
    sig_gates = jax.nn.sigmoid(gate_pre[:, :3])
    candidate = jnp.tanh(gate_pre[:, 3])
    c_new = sig_gates[:, 1] * c_prev + sig_gates[:, 0] * candidate
    h_new = sig_gates[:, 2] * jnp.tanh(c_new)
    gate_acts = jnp.concatenate([sig_gates, candidate[:, None]], axis=1)
    return gate_acts, c_new, h_new


def cell_grad(gate_acts, c_prev, c_new, d_hid, d_cell):
    in_gate = gate_acts[:, 0]
    forget = gate_acts[:, 1]
    out_gate = gate_acts[:, 2]
    candidate = gate_acts[:, 3]
    tanh_c = jnp.tanh(c_new)
    d_cell = d_cell + d_hid * out_gate * (1.0 - tanh_c * tanh_c)
    d_gates = jnp.stack([
        d_cell * candidate * in_gate * (1.0 - in_gate),
        d_cell * c_prev * forget * (1.0 - forget),
        d_hid * tanh_c * out_gate * (1.0 - out_gate),
        d_cell * in_gate * (1.0 - candidate * candidate)], axis=1)
    return d_gates, d_cell * forget


def solution(mesh):
    batch_axes = ('part', 'data')
    seq_spec = P(batch_axes, None, 'model')
    state_spec = P(None, batch_axes, 'model')
    weight_spec = P(None, None, None, 'model')
    in_specs = (P(batch_axes, None, None), seq_spec, state_spec, state_spec,
                P(None, None, 'model'), weight_spec, weight_spec, P(None, None, 'model'))
    out_specs = (seq_spec, state_spec, state_spec, P('part', None, 'model'),
                 P(None, 'part', None, 'model'), P(None, 'part', None, 'model'), P(None, 'part', 'model'))

    def local_program(x_seq, gy_seq, h_init, c_init, w_in, w_up, w_rec, gate_bias):
        num_layers = w_rec.shape[0]
        batch_rows = x_seq.shape[0]
        seq_len = x_seq.shape[1]
        hid_full = w_rec.shape[1]
        hid_loc = w_rec.shape[3]
        own_index = lax.axis_index('model')
        histories = []
        act_store = []
        cell_store = []
        h_finals = []
        c_finals = []
        y_local = None
        for layer_idx in range(num_layers):
            is_top = layer_idx == num_layers - 1
            if layer_idx == 0:
                pre_gates = jnp.einsum('btd,dgh->tbgh', x_seq, w_in, preferred_element_type=jnp.float32)
            else:
                pre_gates = jnp.einsum('tbk,kgh->tbgh', histories[-1][1:], w_up[layer_idx - 1], preferred_element_type=jnp.float32)
            pre_gates = pre_gates + gate_bias[layer_idx]
            w_layer = w_rec[layer_idx]
            hist_len = seq_len if is_top else seq_len + 1
            history = jnp.zeros((hist_len, batch_rows, hid_full), jnp.bfloat16)
            act_buf = jnp.zeros((seq_len, batch_rows, 4, hid_loc), jnp.float32)
            cell_hist = jnp.zeros((seq_len + 1, batch_rows, hid_loc), jnp.float32)
            cell_hist = lax.dynamic_update_index_in_dim(cell_hist, c_init[layer_idx], 0, 0)

            def fwd_step(step_idx, loop_state):
                h_loc, c_loc, history, act_buf, cell_hist = loop_state
                h_full = lax.all_gather(h_loc.astype(jnp.bfloat16), 'model', axis=1, tiled=True)
                gate_pre = pre_gates[step_idx] + jnp.einsum('bk,kgh->bgh', h_full, w_layer, preferred_element_type=jnp.float32)
                gate_acts, c_new, h_new = lstm_cell(gate_pre, c_loc)
                history = lax.dynamic_update_index_in_dim(history, h_full, step_idx, 0)
                act_buf = lax.dynamic_update_index_in_dim(act_buf, gate_acts, step_idx, 0)
                cell_hist = lax.dynamic_update_index_in_dim(cell_hist, c_new, step_idx + 1, 0)
                return (h_new, c_new, history, act_buf, cell_hist)

            h_fin, c_fin, history, act_buf, cell_hist = lax.fori_loop(
                0, seq_len, fwd_step, (h_init[layer_idx], c_init[layer_idx], history, act_buf, cell_hist))
            if is_top:
                own_prev = lax.dynamic_slice_in_dim(history[1:], own_index * hid_loc, hid_loc, axis=2)
                y_time = jnp.concatenate([own_prev, h_fin.astype(jnp.bfloat16)[None]], axis=0)
                y_local = jnp.swapaxes(y_time, 0, 1)
            else:
                last_full = lax.all_gather(h_fin.astype(jnp.bfloat16), 'model', axis=1, tiled=True)
                history = lax.dynamic_update_index_in_dim(history, last_full, seq_len, 0)
            histories.append(history)
            act_store.append(act_buf)
            cell_store.append(cell_hist)
            h_finals.append(h_fin)
            c_finals.append(c_fin)

        dw_in = None
        dw_up_list = []
        dw_rec_list = []
        bias_list = []
        upstream = None
        for layer_idx in reversed(range(num_layers)):
            is_top = layer_idx == num_layers - 1
            w_layer = w_rec[layer_idx]
            act_buf = act_store[layer_idx]
            cell_hist = cell_store[layer_idx]
            incoming = upstream

            def grad_step(step_idx, d_rec, d_cell, bias_acc, dgate_buf):
                if is_top:
                    d_out = lax.dynamic_index_in_dim(gy_seq, step_idx, axis=1, keepdims=False).astype(jnp.float32)
                else:
                    d_out = incoming[step_idx]
                d_gates, d_cell = cell_grad(act_buf[step_idx], cell_hist[step_idx], cell_hist[step_idx + 1], d_out + d_rec, d_cell)
                gates_low = d_gates.astype(jnp.bfloat16)
                dgate_buf = lax.dynamic_update_index_in_dim(dgate_buf, gates_low, step_idx, 0)
                return gates_low, d_cell, bias_acc + jnp.sum(d_gates, axis=0), dgate_buf

            def bwd_step(back_idx, loop_state):
                d_rec, d_cell, bias_acc, dgate_buf = loop_state
                gates_low, d_cell, bias_acc, dgate_buf = grad_step(seq_len - 1 - back_idx, d_rec, d_cell, bias_acc, dgate_buf)
                rec_part = jnp.einsum('bgh,kgh->bk', gates_low, w_layer, preferred_element_type=jnp.float32)
                d_rec = lax.psum_scatter(rec_part, 'model', scatter_dimension=1, tiled=True)
                return (d_rec, d_cell, bias_acc, dgate_buf)

            zero_state = jnp.zeros((batch_rows, hid_loc), jnp.float32)
            start_state = (zero_state, zero_state, jnp.zeros((4, hid_loc), jnp.float32),
                           jnp.zeros((seq_len, batch_rows, 4, hid_loc), jnp.bfloat16))
            d_rec, d_cell, bias_acc, dgate_buf = lax.fori_loop(0, seq_len - 1, bwd_step, start_state)
            outcome = grad_step(0, d_rec, d_cell, bias_acc, dgate_buf)
            bias_list.append(outcome[2])
            dgate_buf = outcome[3]
            dw_rec_list.append(jnp.einsum('tbk,tbgh->kgh', histories[layer_idx][:seq_len], dgate_buf, preferred_element_type=jnp.float32))
            if layer_idx == 0:
                dw_in = jnp.einsum('btd,tbgh->dgh', x_seq, dgate_buf, preferred_element_type=jnp.float32)
            else:
                dw_up_list.append(jnp.einsum('tbk,tbgh->kgh', histories[layer_idx - 1][1:], dgate_buf, preferred_element_type=jnp.float32))
                in_part = jnp.einsum('tbgh,kgh->tbk', dgate_buf, w_up[layer_idx - 1], preferred_element_type=jnp.float32)
                upstream = lax.psum_scatter(in_part, 'model', scatter_dimension=2, tiled=True)
        grad_sums = lax.psum((dw_in, jnp.stack(dw_up_list[::-1]), jnp.stack(dw_rec_list[::-1]), jnp.stack(bias_list[::-1])), 'data')
        return (y_local, jnp.stack(h_finals), jnp.stack(c_finals)) + tuple(grad_sums)

    return jax.shard_map(local_program, mesh=mesh, in_specs=in_specs, out_specs=out_specs, check_vma=False)
```

profile of v0, /device:TPU:0, one launch (start us, length us, event | category | flops | bytes accessed | tf_op | source)
XLA Modules:
  0.0 12780.3 jit_solution(10853733707670244291)
XLA Ops:
  51.5 1734.6 %while.94 = (s32[]{:T(128)}, f32[4,512]{1,0:T(4,128)S(1)}, f32[4,512]{1,0:T(4,128)S(1)}, bf16[129,4,2048]{2,1,0:T(4,128)(2,1)}, f32[128,4,4,512]{3,1,2,0:T(4,128...) while((s32[]{:T(128)}, f32[4,512]{1,0:T(4,128)S(1)}, ...), condition=%wide.region_1.2_spmd, body=%wide.region_0.1_spmd.sunk | while | flops 33599488 | bytes 8741031 | solution.py:78
  1812.8 1858.1 %while.95 = (s32[]{:T(128)}, f32[4,512]{1,0:T(4,128)S(1)}, f32[4,512]{1,0:T(4,128)S(1)}, bf16[128,4,2048]{2,1,0:T(4,128)(2,1)}, f32[128,4,4,512]{3,1,2,0:T(4,128...) while((s32[]{:T(128)}, f32[4,512]{1,0:T(4,128)S(1)}, ...), condition=%wide.region_3.4_spmd, body=%wide.region_2.3_spmd.sunk | while | flops 33599488 | bytes 8806567 | solution.py:78
  3674.0 3635.1 %while.96 = (s32[]{:T(128)}, f32[4,512]{1,0:T(4,128)S(1)}, f32[4,512]{1,0:T(4,128)S(1)}, f32[4,512]{1,0:T(4,128)S(1)}, bf16[128,4,4,512]{3,1,2,0:T(4,128)(2,1)},...) while((s32[]{:T(128)}, f32[4,512]{1,0:T(4,128)S(1)}, ...), condition=%wide.region_7.8_spmd.clone, body=%wide.region_4.7_spmd.clone.sunk | while | flops 33787916 | bytes 10187089 | solution.py:125
  3683.0 18.6 reduce-scatter.14.cloned.1.call-done
  7364.7 3833.8 %while.97 = (s32[]{:T(128)}, f32[4,512]{1,0:T(4,128)S(1)}, f32[4,512]{1,0:T(4,128)S(1)}, f32[4,512]{1,0:T(4,128)S(1)}, bf16[128,4,4,512]{3,1,2,0:T(4,128)(2,1)},...) while((s32[]{:T(128)}, f32[4,512]{1,0:T(4,128)S(1)}, ...), condition=%wide.region_12.13_spmd.clone, body=%wide.region_9.12_spmd.clone.sunk | while | flops 33785868 | bytes 10207569 | solution.py:125
  8944.1 18.6 reduce-scatter.16.cloned.1.call-done
  8974.4 18.6 reduce-scatter.16.cloned.1.call-done
  9004.6 18.6 reduce-scatter.16.cloned.1.call-done
  9034.8 18.6 reduce-scatter.16.cloned.1.call-done
  9065.0 18.6 reduce-scatter.16.cloned.1.call-done
  9095.2 18.6 reduce-scatter.16.cloned.1.call-done
  9125.4 18.6 reduce-scatter.16.cloned.1.call-done
  9155.5 18.6 reduce-scatter.16.cloned.1.call-done
  9185.7 18.6 reduce-scatter.16.cloned.1.call-done
  9215.9 18.6 reduce-scatter.16.cloned.1.call-done
  9246.1 18.6 reduce-scatter.16.cloned.1.call-done
  9276.3 18.6 reduce-scatter.16.cloned.1.call-done
  9306.5 18.6 reduce-scatter.16.cloned.1.call-done
  9397.1 18.6 reduce-scatter.16.cloned.1.call-done
  9517.9 18.6 reduce-scatter.16.cloned.1.call-done
  9638.7 18.6 reduce-scatter.16.cloned.1.call-done
  9970.9 18.6 reduce-scatter.16.cloned.1.call-done
  10091.7 18.6 reduce-scatter.16.cloned.1.call-done
  10212.5 18.6 reduce-scatter.16.cloned.1.call-done
  10544.7 18.6 reduce-scatter.16.cloned.1.call-done
  10665.4 18.6 reduce-scatter.16.cloned.1.call-done
  10786.2 18.6 reduce-scatter.16.cloned.1.call-done
  11118.4 18.6 reduce-scatter.16.cloned.1.call-done
  11262.1 1431.6 %all-reduce.5.cloned.1.call-done = (f32[2048,4,512]{0,2,1:T(8,128)}, f32[1,2048,4,512]{3,1,2,0:T(8,128)}, f32[2,2048,4,512]{3,1,2,0:T(8,128)}) async-done(((f32[2048,4,512]{0,2,1:T(8,128)}, f32[1,2048,4,512]{3,1,2,0:T(8,128)}, f32[2,2048,4,512]{3,1,2,0:T(8,128)}), (f32[2048,4,512]{0,2,1:T(8,128)}, f32[1,2048,4,512]{3,1,2,0:T(8,128)}, f32[2,2048,4,512]{3,1,2,0:T(8,128)})) %all-reduce.5.cloned.1.call-update) | async-done | bytes 67108880 | tf_op jit(solution)/shard_map/psum | solution.py:136
  12693.7 19.8 copy.85
  12713.5 20.9 copy.86
  12734.4 38.0 copy.87
  (5412 shorter events, 10785.7 us)
Async XLA Ops:
  7309.2 52.3 reduce-scatter.12.cloned.1.call-start
  8933.6 29.2 reduce-scatter.16.cloned.1.call-start
  8963.8 29.2 reduce-scatter.16.cloned.1.call-start
  9024.2 29.1 reduce-scatter.16.cloned.1.call-start
  9054.4 29.1 reduce-scatter.16.cloned.1.call-start
  9084.6 29.1 reduce-scatter.16.cloned.1.call-start
  9114.8 29.1 reduce-scatter.16.cloned.1.call-start
  9145.0 29.1 reduce-scatter.16.cloned.1.call-start
  9205.4 29.1 reduce-scatter.16.cloned.1.call-start
  9235.6 29.1 reduce-scatter.16.cloned.1.call-start
  9265.8 29.1 reduce-scatter.16.cloned.1.call-start
  9296.0 29.1 reduce-scatter.16.cloned.1.call-start
  9326.2 29.1 reduce-scatter.16.cloned.1.call-start
  9356.4 29.1 reduce-scatter.16.cloned.1.call-start
  9386.6 29.1 reduce-scatter.16.cloned.1.call-start
  9416.8 29.1 reduce-scatter.16.cloned.1.call-start
  9447.0 29.1 reduce-scatter.16.cloned.1.call-start
  9477.2 29.1 reduce-scatter.16.cloned.1.call-start
  9507.4 29.1 reduce-scatter.16.cloned.1.call-start
  9537.6 29.1 reduce-scatter.16.cloned.1.call-start
  9567.8 29.1 reduce-scatter.16.cloned.1.call-start
  9598.0 29.1 reduce-scatter.16.cloned.1.call-start
  9628.2 29.1 reduce-scatter.16.cloned.1.call-start
  9658.4 29.1 reduce-scatter.16.cloned.1.call-start
  9688.6 29.1 reduce-scatter.16.cloned.1.call-start
  9718.8 29.1 reduce-scatter.16.cloned.1.call-start
  9779.2 29.1 reduce-scatter.16.cloned.1.call-start
  9809.4 29.1 reduce-scatter.16.cloned.1.call-start
  9839.6 29.1 reduce-scatter.16.cloned.1.call-start
  9869.8 29.1 reduce-scatter.16.cloned.1.call-start
  9900.0 29.1 reduce-scatter.16.cloned.1.call-start
  11198.5 1495.2 %all-reduce.5.cloned.1.call-start = ((), (), s32[]{:S(2)}) async-start(), calls=%async_computation.4 | async-start | bytes 134217728 | tf_op jit(solution)/shard_map/psum | solution.py:136
  (234 other events, 6457.9 us)
Sparse Core Ops, SparseCore 0:
  3682.4 19.1 reduce-scatter.13
  8943.6 19.1 reduce-scatter.15
  8973.8 19.1 reduce-scatter.15
  9004.0 19.1 reduce-scatter.15
  9034.2 19.1 reduce-scatter.15
  9064.4 19.1 reduce-scatter.15
  9094.6 19.1 reduce-scatter.15
  9124.8 19.1 reduce-scatter.15
  9155.0 19.1 reduce-scatter.15
  9185.2 19.1 reduce-scatter.15
  9215.4 19.1 reduce-scatter.15
  9245.6 19.1 reduce-scatter.15
  9275.8 19.1 reduce-scatter.15
  9306.0 19.1 reduce-scatter.15
  9336.2 19.1 reduce-scatter.15
  9366.4 19.1 reduce-scatter.15
  9396.6 19.1 reduce-scatter.15
  9426.8 19.1 reduce-scatter.15
  9457.0 19.1 reduce-scatter.15
  9487.2 19.1 reduce-scatter.15
  9517.4 19.1 reduce-scatter.15
  9547.6 19.1 reduce-scatter.15
  9577.8 19.1 reduce-scatter.15
  9608.0 19.1 reduce-scatter.15
  9638.2 19.1 reduce-scatter.15
  9668.4 19.1 reduce-scatter.15
  9698.6 19.1 reduce-scatter.15
  9728.8 19.1 reduce-scatter.15
  9759.0 19.1 reduce-scatter.15
  9789.1 19.1 reduce-scatter.15
  9819.3 19.1 reduce-scatter.15
  9849.5 19.1 reduce-scatter.15
  (222 shorter events, 4229.3 us)
Sparse Core Ops, SparseCore 1:
  7323.2 38.2 reduce-scatter.11
  11241.9 1451.7 all-reduce.4
where the time goes:
time: 12900 us; the launch traced here: 12800 us
  waiting for transfers between devices  6170 us (48%)
  matrix products  2950 us (23%)
  blocking collectives  1980 us (15%)
  local copies, waits for them, and re-layouts  997 us (8%)
  other arithmetic  641 us (5%)
    while x508, waiting for transfers between devices  4730 us
    all_gather x256, blocking collectives, fwd_step(): lax.all_gather(h_loc.astype(jnp.bfloat16), 'model', axis=1, tiled=True)  1960 us
    dot_general x254, matrix products, bwd_step(): jnp.einsum('bgh,kgh->bk', gates_low, w_layer, preferred_element_type=jnp....  1710 us
    psum x1, waiting for transfers between devices, local_program(): lax.psum((dw_in, jnp.stack(dw_up_list[::-1]), jnp.stack(dw_rec_list[::-1]...  1430 us
    dot_general x256, matrix products, fwd_step(): jnp.einsum('bk,kgh->bgh', h_full, w_layer, preferred_element_type=jnp.flo...  1170 us
    another operation x512, other arithmetic, cell_grad(): jnp.stack([d_cell * candidate * in_gate * (1.0 - in_gate), d_cell * c_pre...  276 us
    while x254, local copies, waits for them, and re-layouts  268 us

commit v1 on v0

v1 whole, which is shorter than its diff:
```python
import jax
import jax.numpy as jnp
from jax import lax
from jax.experimental import pallas as pl
from jax.experimental.pallas import tpu as pltpu
from jax.sharding import PartitionSpec as P

MESH = pl.DeviceIdType.MESH
F32 = jnp.float32
BF16 = jnp.bfloat16
CHUNK = 8
PAIRS = CHUNK // 2
ROWS = 4 * CHUNK
VMEM_LIMIT = 60 * 1024 * 1024


def sigm(v):
    return 0.5 * jnp.tanh(0.5 * v) + 0.5


def mm(a, b):
    return jnp.dot(a, b, preferred_element_type=F32)


def place():
    y = lax.axis_index('data')
    m = lax.axis_index('model')
    return y, m, m // 2, m % 2


def dev(y, m):
    return (lax.axis_index('part'), y, m)


def flips(m):
    x = m // 2
    c = m % 2
    return 2 * x + (1 - c), 2 * (1 - x) + c, 2 * (1 - x) + (1 - c)


def remote(src, dst, ssem, rsem, device):
    return pltpu.make_async_remote_copy(src, dst, ssem, rsem, device_id=device, device_id_type=MESH)


def entry_barrier(y, m):
    barrier = pltpu.get_barrier_semaphore()
    for other in flips(m):
        pl.semaphore_signal(barrier, inc=1, device_id=dev(y, other), device_id_type=MESH)
    pl.semaphore_wait(barrier, 3)


def fwd_kernel(wa_hbm, wb_hbm, wup_hbm, prea_hbm, preb_hbm, bias_ref, h0_ref, c0_ref,
               act_hbm, cell_hbm, hist_hbm, hfin_ref, cfin_ref,
               w, wup, prea, preb, actv, cellv, histv, hbuf, hch, cst, hs, hr, pout,
               lsem, osem, xs, xr, hss, hrs, ps, prs):
    y, m, x, c = place()
    beside, across, skew = flips(m)
    nch = hbuf.shape[0]
    hl = hs.shape[3]
    half = 2 * hl
    wide = 4 * hl
    own_cols = pl.ds(pl.multiple_of(c * half, half), half)

    loads = []
    for pos, shard in enumerate((m, across, beside, skew)):
        rows = pl.ds(pl.multiple_of(shard * hl, hl), hl)
        for col, src in enumerate((wa_hbm, wb_hbm)):
            loads.append(pltpu.make_async_copy(
                src.at[rows, :], w.at[pl.ds(pos * hl, hl), pl.ds(col * wide, wide)], lsem.at[len(loads)]))
    for pos, shard in enumerate((0, 2, 1, 3)):
        loads.append(pltpu.make_async_copy(
            wup_hbm.at[pl.ds(shard * hl, hl), :], wup.at[pl.ds(pos * hl, hl), :], lsem.at[len(loads)]))
    for cp in loads:
        cp.start()

    @pl.when(x == 0)
    def _():
        one = pltpu.make_async_copy(prea_hbm, prea, lsem.at[12])
        two = pltpu.make_async_copy(preb_hbm, preb, lsem.at[13])
        one.start()
        two.start()
        one.wait()
        two.wait()

    entry_barrier(y, m)

    def swap(slot, s):
        return remote(hs.at[slot, s], hr.at[slot, s], xs.at[slot, s], xr.at[slot, s], dev(y, beside))

    def hsend(k, dest, i):
        return remote(histv.at[k], hbuf.at[k, :, own_cols], hss.at[i], hrs.at[k, c], dev(y, dest))

    def hrecv(k, core):
        cols = pl.ds(pl.multiple_of(core * half, half), half)
        return remote(histv.at[k], hbuf.at[k, :, cols], hss.at[0], hrs.at[k, core], dev(y, beside))

    def psend(k):
        return remote(pout, preb.at[pl.ds(k * PAIRS, PAIRS)], ps.at[0], prs.at[k], dev(y, across))

    cst[...] = c0_ref[...]
    cellv[0, 0:4, :] = c0_ref[...]
    cellv[0, 4:8, :] = c0_ref[...]
    for s in (0, 1):
        hs[0, s] = h0_ref[:, s * hl:(s + 1) * hl].astype(BF16)
        swap(0, s).start()
    for cp in loads:
        cp.wait()

    def step(k, p, j):
        pair = k * PAIRS + p
        rows = slice(4 * j, 4 * j + 4)
        cols = (slice(0, wide), slice(wide, 2 * wide))
        acc = [mm(hs[j, 0], w[0:hl, cols[s]]) + mm(hs[j, 1], w[hl:half, cols[s]]) for s in (0, 1)]
        swap(j, 0).wait()
        swap(j, 1).wait()
        got = (hr[j, 0], hr[j, 1])
        acc = [acc[s] + (mm(got[0], w[half:half + hl, cols[s]]) + mm(got[1], w[half + hl:, cols[s]])) for s in (0, 1)]
        for s, pre in ((0, prea), (1, preb)):
            base = s * wide
            units = slice(s * hl, (s + 1) * hl)

            def gate(g):
                return acc[s][:, g * hl:(g + 1) * hl] + pre[pair, rows, g * hl:(g + 1) * hl]

            gi = sigm(gate(0))
            gf = sigm(gate(1))
            go = sigm(gate(2))
            gu = jnp.tanh(gate(3))
            cn = gf * cst[:, units] + gi * gu
            hn = go * jnp.tanh(cn)
            hs[1 - j, s] = hn.astype(BF16)
            cst[:, units] = cn
            for g, val in enumerate((gi, gf, go, gu)):
                actv[pair, rows, base + g * hl:base + (g + 1) * hl] = val
            cellv[pair + 1, rows, units] = cn
            hch[p, rows, units] = hn
        swap(1 - j, 0).start()
        swap(1 - j, 1).start()

    def up_product(k):
        return (mm(hbuf[k], wup[...]) + bias_ref[...]).reshape(PAIRS, 8, wide)

    def act_out(k):
        rows = pl.ds(k * PAIRS, PAIRS)
        return pltpu.make_async_copy(actv.at[rows], act_hbm.at[rows], osem.at[0])

    def slot_body(s, _):
        k = s - x
        live = (k >= 0) & (k < nch)

        @pl.when((x == 1) & (s >= 1))
        def _():
            hrecv(k, 0).wait_recv()
            hrecv(k, 1).wait_recv()
            prea[pl.ds(k * PAIRS, PAIRS)] = up_product(k)
            psend(k).wait_recv()

        def pair_body(p, _):
            @pl.when((x == 0) & (s >= 1) & (p == 1))
            def _():
                hrecv(s - 1, 1 - c).wait_recv()

                @pl.when(s >= 2)
                def _():
                    psend(s - 2).wait_send()

                pout[...] = up_product(s - 1)
                psend(s - 1).start()

            @pl.when(live)
            def _():
                step(k, p, 0)
                step(k, p, 1)
            return 0

        lax.fori_loop(0, PAIRS, pair_body, 0)

        @pl.when(live)
        def _():
            block = hch[...].reshape(ROWS, half).astype(BF16)
            histv[k] = block
            act_out(k).start()

            @pl.when(x == 0)
            def _():
                hbuf[k, :, own_cols] = block

                @pl.when(k >= 1)
                def _():
                    for i, dest in enumerate((beside, across, skew)):
                        hsend(k - 1, dest, i).wait_send()
                for i, dest in enumerate((beside, across, skew)):
                    hsend(k, dest, i).start()
        return 0

    lax.fori_loop(0, nch + 1, slot_body, 0)
    swap(0, 0).wait()
    swap(0, 1).wait()
    outs = (pltpu.make_async_copy(histv, hist_hbm, osem.at[1]),
            pltpu.make_async_copy(cellv, cell_hbm, osem.at[2]))
    for cp in outs:
        cp.start()

    @pl.when(x == 0)
    def _():
        for i, dest in enumerate((beside, across, skew)):
            hsend(nch - 1, dest, i).wait_send()
        psend(nch - 1).wait_send()

    hfin_ref[...] = hch[PAIRS - 1, 4:8, :]
    cfin_ref[...] = cst[...]
    for cp in outs:
        cp.wait()
    pltpu.make_async_copy(actv, act_hbm, osem.at[0]).wait()


def bwd_kernel(wta_hbm, wtb_hbm, wupt_hbm, act_hbm, cell_hbm, gy_hbm,
               dg_hbm, dgo_hbm, bias_ref,
               wt, wupt, actv, cellv, dout, dgv, dgr, dgch, dgs, dct, bacc, own, snd, rcv, pin, pout,
               lsem, asem, osem, xs, xr, gs, grs, ps, prs):
    y, m, x, c = place()
    beside, across, skew = flips(m)
    nch = dgv.shape[0]
    half = own.shape[1]
    hl = half // 2
    wide = 4 * hl

    loads = []
    for pos, shard in enumerate((beside, skew, m, across)):
        cols = pl.ds(pl.multiple_of(shard * hl, hl), hl)
        for row, src in enumerate((wta_hbm, wtb_hbm)):
            loads.append(pltpu.make_async_copy(
                src.at[:, cols], wt.at[pl.ds(row * wide, wide), pl.ds(pos * hl, hl)], lsem.at[len(loads)]))
    for pos, shard in enumerate((1 - c, 3 - c, c, 2 + c)):
        cols = pl.ds(pl.multiple_of(shard * hl, hl), hl)
        loads.append(pltpu.make_async_copy(
            wupt_hbm.at[:, cols], wupt.at[:, pl.ds(pos * hl, hl)], lsem.at[len(loads)]))
    loads.append(pltpu.make_async_copy(cell_hbm, cellv, lsem.at[12]))
    for cp in loads:
        cp.start()

    @pl.when(x == 1)
    def _():
        one = pltpu.make_async_copy(gy_hbm, dout, lsem.at[13])
        one.start()
        one.wait()

    def act_in(k):
        rows = pl.ds(k * PAIRS, PAIRS)
        return pltpu.make_async_copy(act_hbm.at[rows], actv.at[rows], asem.at[k])

    def start_act(i, _):
        act_in(nch - 1 - i).start()
        return 0

    lax.fori_loop(0, nch, start_act, 0)
    entry_barrier(y, m)

    def swap(slot):
        return remote(snd.at[slot], rcv.at[slot], xs.at[slot], xr.at[slot], dev(y, beside))

    def gsend(k):
        return remote(dgv.at[k, :, pl.ds(wide, wide)], dgr.at[k], gs.at[0], grs.at[k], dev(y, across))

    def psend(k, pos, dest, src):
        return remote(pout.at[pos], pin.at[src, k], ps.at[pos], prs.at[src, k], dev(y, dest))

    dgs[...] = jnp.zeros(dgs.shape, BF16)
    dct[...] = jnp.zeros(dct.shape, F32)
    bacc[...] = jnp.zeros(bacc.shape, F32)
    for cp in loads:
        cp.wait()

    def step(k, p, j):
        pair = k * PAIRS + p
        rows = slice(4 * j, 4 * j + 4)
        dgl = dgs[...]
        snd[j] = mm(dgl, wt[:, 0:half])
        swap(j).start()
        own[...] = mm(dgl, wt[:, half:])
        swap(j).wait()
        for s in (0, 1):
            base = s * wide
            units = slice(s * hl, (s + 1) * hl)
            gi, gf, go, gu = (actv[pair, rows, base + g * hl:base + (g + 1) * hl] for g in range(4))
            tc = jnp.tanh(cellv[pair + 1, rows, units])
            cp = cellv[pair + 1, 0:4, units] if j else cellv[pair, 4:8, units]
            dh = dout[pair, rows, units] + own[:, units] + rcv[j, :, units]
            dc = dct[:, units] + dh * go * (1.0 - tc * tc)
            dct[:, units] = dc * gf
            grads = (dc * gu * gi * (1.0 - gi), dc * cp * gf * (1.0 - gf),
                     dh * tc * go * (1.0 - go), dc * gi * (1.0 - gu * gu))
            for g, val in enumerate(grads):
                cols = slice(base + g * hl, base + (g + 1) * hl)
                bacc[:, cols] += val
                dgs[:, cols] = val.astype(BF16)
                dgch[p, rows, cols] = val

    def slot_body(s, _):
        k = nch - 1 - s + (1 - x)
        live = (k >= 0) & (k < nch)

        @pl.when(live)
        def _():
            act_in(k).wait()

        @pl.when((x == 0) & live)
        def _():
            gsend(k).wait_recv()
            block = dgr[k]

            @pl.when(s >= 2)
            def _():
                psend(k + 1, 0, beside, 2).wait_send()
            pout[0] = mm(block, wupt[:, 0:half]).reshape(PAIRS, 8, half)
            psend(k, 0, beside, 2).start()
            part = mm(block, wupt[:, half:]).reshape(PAIRS, 8, half)
            for src in (0, 1, 2):
                psend(k, 0, beside, src).wait_recv()
            dout[pl.ds(k * PAIRS, PAIRS)] = part + pin[0, k] + pin[1, k] + pin[2, k]

        @pl.when(live)
        def _():
            def pair_body(i, _):
                step(k, PAIRS - 1 - i, 1)
                step(k, PAIRS - 1 - i, 0)
                return 0

            lax.fori_loop(0, PAIRS, pair_body, 0)
            dgv[k] = dgch[...].reshape(ROWS, 2 * wide).astype(BF16)

        @pl.when((x == 1) & live)
        def _():
            @pl.when(s >= 1)
            def _():
                gsend(k + 1).wait_send()
                psend(k + 1, 0, skew, c).wait_send()
                psend(k + 1, 1, across, c).wait_send()
            gsend(k).start()
            block = dgv[k, :, 0:wide]
            pout[0] = mm(block, wupt[:, 0:half]).reshape(PAIRS, 8, half)
            psend(k, 0, skew, c).start()
            pout[1] = mm(block, wupt[:, half:]).reshape(PAIRS, 8, half)
            psend(k, 1, across, c).start()
        return 0

    lax.fori_loop(0, nch + 1, slot_body, 0)
    outs = (pltpu.make_async_copy(dgv, dg_hbm, osem.at[0]),
            pltpu.make_async_copy(dgr, dgo_hbm, osem.at[1]))
    for cp in outs:
        cp.start()
    bias_ref[...] = bacc[...]

    @pl.when(x == 0)
    def _():
        psend(0, 0, beside, 2).wait_send()

    @pl.when(x == 1)
    def _():
        gsend(0).wait_send()
        psend(0, 0, skew, c).wait_send()
        psend(0, 1, across, c).wait_send()
    for cp in outs:
        cp.wait()


def any_spec():
    return pl.BlockSpec(memory_space=pl.ANY)


def vmem_spec():
    return pl.BlockSpec(memory_space=pltpu.VMEM)


def sds(shape, dtype):
    return jax.ShapeDtypeStruct(shape, dtype)


def run_fwd(wa, wb, wup, prea, preb, bias, h0, c0):
    hidden, wide = wa.shape
    hl = wide // 4
    half = 2 * hl
    npair = prea.shape[0]
    nch = npair // PAIRS
    dma = pltpu.SemaphoreType.DMA
    return pl.pallas_call(
        fwd_kernel,
        name='lstm_forward',
        out_shape=(sds((npair, 8, 2 * wide), F32), sds((npair + 1, 8, half), F32),
                   sds((nch, ROWS, half), BF16), sds((4, half), F32), sds((4, half), F32)),
        in_specs=[any_spec()] * 5 + [vmem_spec()] * 3,
        out_specs=(any_spec(), any_spec(), any_spec(), vmem_spec(), vmem_spec()),
        scratch_shapes=[
            pltpu.VMEM((hidden, 2 * wide), BF16), pltpu.VMEM((hidden, wide), BF16),
            pltpu.VMEM((npair, 8, wide), F32), pltpu.VMEM((npair, 8, wide), F32),
            pltpu.VMEM((npair, 8, 2 * wide), F32), pltpu.VMEM((npair + 1, 8, half), F32),
            pltpu.VMEM((nch, ROWS, half), BF16), pltpu.VMEM((nch, ROWS, hidden), BF16),
            pltpu.VMEM((PAIRS, 8, half), F32), pltpu.VMEM((4, half), F32),
            pltpu.VMEM((2, 2, 4, hl), BF16), pltpu.VMEM((2, 2, 4, hl), BF16),
            pltpu.VMEM((PAIRS, 8, wide), F32),
            dma((14,)), dma((3,)), dma((2, 2)), dma((2, 2)), dma((3,)), dma((nch, 2)), dma((1,)), dma((nch,)),
        ],
        compiler_params=pltpu.CompilerParams(collective_id=0, has_side_effects=True, vmem_limit_bytes=VMEM_LIMIT),
    )(wa, wb, wup, prea, preb, bias, h0, c0)


def run_bwd(wta, wtb, wupt, act, cell, gy):
    wide, hidden = wta.shape
    hl = wide // 4
    half = 2 * hl
    npair = act.shape[0]
    nch = npair // PAIRS
    dma = pltpu.SemaphoreType.DMA
    return pl.pallas_call(
        bwd_kernel,
        name='lstm_backward',
        out_shape=(sds((nch, ROWS, 2 * wide), BF16), sds((nch, ROWS, wide), BF16), sds((4, 2 * wide), F32)),
        in_specs=[any_spec()] * 6,
        out_specs=(any_spec(), any_spec(), vmem_spec()),
        scratch_shapes=[
            pltpu.VMEM((2 * wide, hidden), BF16), pltpu.VMEM((wide, hidden), BF16),
            pltpu.VMEM((npair, 8, 2 * wide), F32), pltpu.VMEM((npair + 1, 8, half), F32),
            pltpu.VMEM((npair, 8, half), F32),
            pltpu.VMEM((nch, ROWS, 2 * wide), BF16), pltpu.VMEM((nch, ROWS, wide), BF16),
            pltpu.VMEM((PAIRS, 8, 2 * wide), F32), pltpu.VMEM((4, 2 * wide), BF16),
            pltpu.VMEM((4, half), F32), pltpu.VMEM((4, 2 * wide), F32),
            pltpu.VMEM((4, half), F32), pltpu.VMEM((2, 4, half), F32), pltpu.VMEM((2, 4, half), F32),
            pltpu.VMEM((3, nch, PAIRS, 8, half), F32), pltpu.VMEM((2, PAIRS, 8, half), F32),
            dma((14,)), dma((nch,)), dma((2,)), dma((2,)), dma((2,)), dma((1,)), dma((nch,)), dma((2,)), dma((3, nch)),
        ],
        compiler_params=pltpu.CompilerParams(collective_id=1, has_side_effects=True, vmem_limit_bytes=VMEM_LIMIT),
    )(wta, wtb, wupt, act, cell, gy)


ACROSS = [(0, 2), (1, 3), (2, 0), (3, 1)]


def solution(mesh):
    batch_axes = ('part', 'data')
    seq_spec = P(batch_axes, None, 'model')
    state_spec = P(None, batch_axes, 'model')
    weight_spec = P(None, None, None, 'model')
    in_specs = (P(batch_axes, None, None), seq_spec, state_spec, state_spec,
                P(None, None, 'model'), weight_spec, weight_spec, P(None, None, 'model'))
    out_specs = (seq_spec, state_spec, state_spec, P('part', None, 'model'),
                 P(None, 'part', None, 'model'), P(None, 'part', None, 'model'), P(None, 'part', 'model'))

    def local_program(x_seq, gy_seq, h_init, c_init, w_in, w_up, w_rec, gate_bias):
        rows, seq_len, width = x_seq.shape
        hl = w_in.shape[2]
        wide = 4 * hl
        half = 2 * hl
        hidden = w_rec.shape[1]
        npair = seq_len // 2
        nch = seq_len // CHUNK
        m = lax.axis_index('model')
        x = m // 2

        def across(v):
            return lax.ppermute(v, 'model', ACROSS)

        def pick(v, i):
            return lax.dynamic_index_in_dim(v, i, 0, keepdims=False)

        wa = pick(w_rec, x)
        wb = across(pick(w_rec, 1 - x))
        wa = wa.reshape(hidden, wide)
        wb = wb.reshape(hidden, wide)
        wup = w_up[0].reshape(hidden, wide)
        xt = jnp.swapaxes(x_seq, 0, 1).reshape(seq_len * rows, width)
        pre = mm(xt, w_in.reshape(width, wide)) + gate_bias[0].reshape(1, wide)
        pre = pre.reshape(npair, 8, wide)
        preb = across(pre)
        h0 = jnp.concatenate([pick(h_init, x), across(pick(h_init, 1 - x))], axis=1)
        c0 = jnp.concatenate([pick(c_init, x), across(pick(c_init, 1 - x))], axis=1)
        act, cell, hist, hfin, cfin = run_fwd(wa, wb, wup, pre, preb, gate_bias[1].reshape(1, wide), h0, c0)

        gy = jnp.concatenate([gy_seq, across(gy_seq)], axis=2)
        gy = jnp.swapaxes(gy, 0, 1).reshape(npair, 8, half).astype(F32)
        dg, dg_up, bias_part = run_bwd(wa.T, wb.T, wup.T, act, cell, gy)

        every = lax.all_gather(hist.reshape(seq_len * 4, half), ('data', 'model'))
        every = every.reshape(2, 4, seq_len, 4, 2, hl)

        def layer_hist(layer):
            a = every[:, 2 * layer:2 * layer + 2]
            first, second = a[..., layer, :], a[..., 1 - layer, :]
            full = jnp.stack([first, second], axis=1)
            return jnp.moveaxis(full.reshape(2, 4, seq_len, 4, hl), 1, 3).reshape(2, seq_len, 4, hidden)

        h_low = layer_hist(0)
        h_top = layer_hist(1)
        init_all = lax.all_gather(h_init.astype(BF16), 'model', axis=2, tiled=True)
        init_all = lax.all_gather(init_all, 'data')

        def shifted(full, layer):
            return jnp.concatenate([init_all[:, layer][:, None], full[:, :-1]], axis=1)

        x_all = lax.all_gather(jnp.swapaxes(x_seq, 0, 1), 'data')
        dg = dg.reshape(seq_len * 4, 2 * wide)
        mine = lax.all_gather(dg[:, :wide], 'data')
        other = lax.all_gather(across(dg[:, wide:]), 'data')
        dg_low = jnp.where(x == 0, mine, other).reshape(-1, wide)
        dg_top = jnp.where(x == 0, other, mine).reshape(-1, wide)

        def outer(a, b):
            return jnp.einsum('rk,rn->kn', a.reshape(-1, a.shape[-1]), b, preferred_element_type=F32)

        dw_in = outer(x_all, dg_low).reshape(width, 4, hl)
        dw_up = outer(h_low, dg_top).reshape(1, hidden, 4, hl)
        dw_rec = jnp.stack([outer(shifted(h_low, 0), dg_low), outer(shifted(h_top, 1), dg_top)])
        dw_rec = dw_rec.reshape(2, hidden, 4, hl)

        bsum = jnp.sum(bias_part, axis=0)
        b_mine = bsum[:wide]
        b_other = across(bsum[wide:])
        bias = jnp.where(x == 0, jnp.stack([b_mine, b_other]), jnp.stack([b_other, b_mine]))
        bias = lax.psum(bias, 'data').reshape(2, 4, hl)

        def both(v):
            mine, other = v[:, :hl], across(v[:, hl:])
            return jnp.where(x == 0, jnp.stack([mine, other]), jnp.stack([other, mine]))

        own_top = lax.dynamic_slice_in_dim(lax.dynamic_index_in_dim(h_top, lax.axis_index('data'), 0, keepdims=False),
                                           m * hl, hl, axis=2)
        y_local = jnp.swapaxes(own_top, 0, 1)
        return (y_local, both(hfin), both(cfin), dw_in, dw_up, dw_rec, bias)

    return jax.shard_map(local_program, mesh=mesh, in_specs=in_specs, out_specs=out_specs, check_vma=False)
```

time: 12900 us -> 1540 us (0.12)
  waiting for transfers between devices: 6170 us -> 262 us
  matrix products: 2950 us -> 68.8 us
  blocking collectives: 1980 us -> 21.3 us
  Pallas kernels: 0 us -> 771 us
  local copies, waits for them, and re-layouts: 997 us -> 341 us
  other arithmetic: 641 us -> 41.5 us
    while x508 -> x0, waiting for transfers between devices: 4730 us -> none
    dot_general x517 -> x5, matrix products: 2950 us -> 68.8 us  [the longest x4 59.3 us: outer(): jnp.einsum('rk,rn->kn', a.reshape(-1, a.shape[-1]), b, preferred_element_...]
    all_gather x257 -> x2, blocking collectives: 1970 us -> 11.5 us  [the longest x1 6.92 us: local_program(): init_all = lax.all_gather(h_init.astype(BF16), 'model', axis=2, tiled=True)]
    psum x1 -> x0, waiting for transfers between devices: 1430 us -> none  [local_program(): lax.psum((dw_in, jnp.stack(dw_up_list[::-1]), jnp.stack(dw_rec_list[::-1]...]
    pallas_call x0 -> x2, Pallas kernels: none -> 771 us  [the longest x1 411 us: run_bwd(): pl.pallas_call(bwd_kernel, name='lstm_backward', out_shape=(sds((nch, ROW...]
    dynamic_update_slice x768 -> x0, other arithmetic: 323 us -> none  [the longest x256 159 us: grad_step(): lax.dynamic_update_index_in_dim(dgate_buf, gates_low, step_idx, 0)]
    while x258 -> x0, local copies, waits for them, and re-layouts: 285 us -> none
    another operation x518 -> x3, other arithmetic: 296 us -> 23.3 us  [the longest x1 18.6 us: local_program(): jnp.stack([outer(shifted(h_low, 0), dg_low), outer(shifted(h_top, 1), dg_...]
where the time goes in v1:
time: 1540 us; the launch traced here: 1530 us
  Pallas kernels  771 us (50%)
  local copies, waits for them, and re-layouts  341 us (22%)
  waiting for transfers between devices  262 us (17%)
  matrix products  68.8 us (4%)
  other arithmetic  41.5 us (3%)
  blocking collectives  21.3 us (1%)
    pallas_call x1, Pallas kernels, run_bwd(): pl.pallas_call(bwd_kernel, name='lstm_backward', out_shape=(sds((nch, ROW...  411 us
    pallas_call x1, Pallas kernels, run_fwd(): pl.pallas_call(fwd_kernel, name='lstm_forward', out_shape=(sds((npair, 8,...  360 us
    ppermute x9, waiting for transfers between devices, across(): return lax.ppermute(v, 'model', ACROSS)  249 us
    unnamed x39, local copies, waits for them, and re-layouts  126 us
    dot_general x4, matrix products, outer(): jnp.einsum('rk,rn->kn', a.reshape(-1, a.shape[-1]), b, preferred_element_...  59.3 us
  transfers between devices with their start and end apart: 13, of which 4 were waited for; matrix products, arithmetic and copies ran while one was open for 12% of the time, Pallas kernels for 50%

profile of v1, /device:TPU:0, one launch (start us, length us, event | category | flops | bytes accessed | tf_op | source)
XLA Modules:
  0.0 1531.3 jit_solution(11058761035203004148)
XLA Ops:
  7.2 15.7 %constant_dynamic-slice_fusion.1 = (bf16[1,2048,4,512]{3,2,1,0:T(4,128)(2,1)}, bf16[1,2048,4,512]{3,2,1,0:T(4,128)(2,1)}) fusion(bf16[2,2048,4,512]{3,2,1,0:T(4,128)(2,1)} %param.14, s32[]{:T(128)S(6)} %select_n.62, s32[]{:T(128)S(6)} %select_n.61), kind=kLoop, calls=%fused_computation.36 | loop fusion | bytes 33554440 | tf_op jit(solution)/shard_map/jit(dynamic_index_in_dim)/dynamic_slice | solution.py:463
  22.9 8.6 copy.157
  40.4 10.4 copy.148
  50.8 9.5 add_bitcast_fusion.prea_hbm
  64.7 13.6 copy.110
  78.3 12.2 copy.115.wa_hbm
  90.5 13.8 copy.113
  104.3 12.3 copy.117.wup_hbm
  117.2 199.5 %collective-permute-done.2 = f32[4,512]{1,0:T(4,128)S(1)} collective-permute-done((f32[4,512]{1,0:T(4,128)S(1)}, f32[4,512]{1,0:T(4,128)S(1)}, u32[]{:S(2)}, u32[]{:S(2)}) %collective-permute-start.2) | collective-permute-done | bytes 8224 | tf_op jit(solution)/shard_map/ppermute | solution.py:460
  321.3 11.3 copy.112
  332.6 12.3 copy.116.wb_hbm
  344.9 359.7 %lstm_forward.1 = (f32[64,8,4096]{2,1,0:T(8,128)}, f32[65,8,1024]{2,1,0:T(8,128)}, bf16[16,32,1024]{2,1,0:T(8,128)(2,1)}, f32[4,1024]{1,0:T(4,128)}, f32[4,1024]{1,0:T(4,128)}) custom-call(bf16[2048,2048]{1,0:T(8,128)(2,1)} %copy.115.wa_hbm, bf16[2048,2048]{1,0:T(8,128)(2,1)} %copy.116.wb_hbm, bf16[2048,2048]{1,0:T(8,128)(2,1)} %copy.117.wup_hbm, ...), custom_call_target="tpu_custom_call" | custom-call | tf_op jit(solution)/shard_map/lstm_forward/pallas_call | solution.py:386
  704.6 411.2 %lstm_backward.1 = (bf16[16,32,4096]{2,1,0:T(8,128)(2,1)}, bf16[16,32,2048]{2,1,0:T(8,128)(2,1)}, f32[4,4096]{1,0:T(4,128)}) custom-call(bf16[2048,2048]{1,0:T(8,128)(2,1)} %bitcast.99, bf16[2048,2048]{1,0:T(8,128)(2,1)} %bitcast.103, bf16[2048,2048]{1,0:T(8,128)(2,1)} %bitcast.101, f32[64,8,4096]{2,1,0:T(8,128)} %get-tuple-element.17.act_hbm, ...), custom_call_target="tpu_custom_call" | custom-call | tf_op jit(solution)/shard_map/lstm_backward/pallas_call | solution.py:414
  1120.7 48.0 %collective-permute-done.7 = bf16[512,2048]{1,0:T(8,128)(2,1)S(1)} collective-permute-done((bf16[512,2048]{1,0:T(8,128)(2,1)}, bf16[512,2048]{1,0:T(8,128)(2,1)S(1)}, u32[]{:S(2)}, u32[]{:S(2)}) %collective-permute-start.7) | collective-permute-done | bytes 2097184 | tf_op jit(solution)/shard_map/ppermute | solution.py:460
  1188.8 7.4 copy.123
  1209.3 9.8 psum.7
  1219.7 11.9 all-gather.13.cloned.1.call-done
  1250.2 15.6 %fusion.3 = f32[2048,2048]{1,0:T(8,128)} fusion(bf16[1024,2048]{1,0:T(8,128)(2,1)} %reshape.105, bf16[1024,2048]{1,0:T(8,128)(2,1)} %all-gather.11.cloned.1.call-done, bf16[1024,2048]{1,0:T(8,128)(2,1)} %all-gather.13.cloned.1.call-done, pred[]{:T(512)S(6)} %eq.2), kind=kOutput, calls=%fused_computation.20 | convolution fusion | flops 8592031744 | bytes 29360128 | tf_op jit(solution)/shard_map/rk,rn->kn/dot_general | solution.py:507
  1265.8 19.8 %copy.137 = f32[2048,4,512]{2,1,0:T(4,128)} copy(f32[2048,4,512]{0,2,1:T(8,128)} %bitcast.109) | data formatting | bytes 33554432
  1285.6 14.4 reshape.100
  1300.0 17.9 %fusion.5 = (bf16[2,2,128,4,1,512]{5,4,3,2,1,0:T(2,128)(2,1)S(1)}, bf16[2,2,128,4,1,512]{5,4,3,2,1,0:T(2,128)(2,1)S(1)}, bf16[2,2,128,4,1,512]{5,4,3,2,1,0:T(2,128)(2,1)}, bf16[2,2,128,4,1,512]{5,4,3,2,1,0:T(2,128)(2,1)}) fusion(bf16[2,4,128,4,2,512]{5,4,3,2,1,0:T(2,128)(2,1)} %reshape.100), kind=kLoop, calls=%fused_computation.38 | loop fusion | bytes 16777216 | tf_op jit(solution)/shard_map/slice | solution.py:487
  1322.7 7.4 copy.129
  1330.2 7.6 copy.126
  1341.4 7.9 copy.131
  1364.5 7.3 copy.120
  1377.7 7.8 copy.135
  1392.4 23.0 %convolution_bitcast_fusion.1 = f32[1,2048,4,512]{3,1,2,0:T(8,128)S(1)} fusion(bf16[4,512,1024]{2,1,0:T(8,128)(2,1)} %bitcast.119, bf16[1024,2048]{1,0:T(8,128)(2,1)} %reshape.110), kind=kOutput, calls=%fused_computation.3 | convolution fusion | flops 8589934592 | bytes 25165824 | tf_op jit(solution)/shard_map/rk,rn->kn/dot_general | solution.py:507
  1415.4 11.7 convolution_bitcast_fusion
  1427.1 18.6 %pad_maximum_fusion = f32[2,2048,4,512]{3,1,2,0:T(8,128)} fusion(f32[1,2048,4,512]{3,1,2,0:T(8,128)} %convolution_bitcast_fusion, f32[1,2048,4,512]{3,1,2,0:T(8,128)S(1)} %convolution_bitcast_fusion.1), kind=kLoop, calls=%fused_computation | loop fusion | flops 8388608 | bytes 67108864 | tf_op jit(solution)/shard_map/stack | solution.py:511
  1445.7 38.4 %copy.139 = f32[2,2048,4,512]{3,2,1,0:T(4,128)} copy(f32[2,2048,4,512]{3,1,2,0:T(8,128)} %pad_maximum_fusion) | data formatting | bytes 67108864
  1487.9 9.0 convolution_bitcast_fusion.2
  1496.8 25.6 %copy.138 = f32[1,2048,4,512]{3,2,1,0:T(4,128)} copy(f32[1,2048,4,512]{3,1,2,0:T(8,128)S(1)} %convolution_bitcast_fusion.2) | data formatting | bytes 33554432
  (97 shorter events, 117.8 us)
Async XLA Ops:
  7.2 1181.7 %all-gather.15.cloned.1.call-start = ((), (), s32[]{:S(2)}) async-start(), calls=%async_computation.3 | async-start | bytes 6291456 | tf_op jit(solution)/shard_map/all_gather | solution.py:499
  22.9 12.0 copy-start.2
  31.5 289.8 %collective-permute-start = (bf16[2048,4,512]{2,0,1:T(8,128)(2,1)}, bf16[2048,4,512]{2,0,1:T(8,128)(2,1)}, u32[]{:S(2)}, u32[]{:S(2)}) collective-permute-start(bf16[2048,4,512]{2,0,1:T(8,128)(2,1)} %bitcast.113), channel_id=1, source_target_pairs={{0,2},{1,3},{2,0},{3,1},{4,6},{5,7},{6,4},{7,5}} | collective-permute-start | bytes 25165832 | tf_op jit(solution)/shard_map/ppermute | solution.py:460
  34.9 5.5 copy-start.10
  50.8 9.8 copy-start.7
  50.8 11.8 copy-start.9
  50.8 11.9 copy-start.11
  60.3 284.6 %collective-permute-start.1 = (f32[64,8,2048]{2,1,0:T(8,128)}, f32[64,8,2048]{2,1,0:T(8,128)}, u32[]{:S(2)}, u32[]{:S(2)}) collective-permute-start(f32[64,8,2048]{2,1,0:T(8,128)} %add_bitcast_fusion.prea_hbm), channel_id=1, source_target_pairs={{0,2},{1,3},{2,0},{3,1},{4,6},{5,7},{6,4},{7,5}} | collective-permute-start | bytes 12582920 | tf_op jit(solution)/shard_map/ppermute | solution.py:460
  60.3 1159.3 %all-gather.11.cloned.1.call-start = ((), (), s32[]{:S(2)}) async-start(), calls=%async_computation.1 | async-start | bytes 6291456 | tf_op jit(solution)/shard_map/all_gather | solution.py:501
  60.6 257.4 %collective-permute-start.6 = (bf16[4,128,512]{2,1,0:T(8,128)(2,1)S(1)}, bf16[4,128,512]{2,1,0:T(8,128)(2,1)S(1)}, u32[]{:S(2)}, u32[]{:S(2)}) collective-permute-start(bf16[4,128,512]{2,1,0:T(8,128)(2,1)S(1)} %copy-done.7), channel_id=1, source_target_pairs={{0,2},{1,3},{2,0},{3,1},{4,6},{5,7},{6,4},{7,5}} | collective-permute-start | bytes 1572872 | tf_op jit(solution)/shard_map/ppermute | solution.py:460
  62.6 254.1 %collective-permute-start.2 = (f32[4,512]{1,0:T(4,128)S(1)}, f32[4,512]{1,0:T(4,128)S(1)}, u32[]{:S(2)}, u32[]{:S(2)}) collective-permute-start(f32[4,512]{1,0:T(4,128)S(1)} %get-tuple-element.77), channel_id=1, source_target_pairs={{0,2},{1,3},{2,0},{3,1},{4,6},{5,7},{6,4},{7,5}} | collective-permute-start | bytes 24584 | tf_op jit(solution)/shard_map/ppermute | solution.py:460
  62.7 254.6 %collective-permute-start.3 = (f32[4,512]{1,0:T(4,128)S(1)}, f32[4,512]{1,0:T(4,128)S(1)}, u32[]{:S(2)}, u32[]{:S(2)}) collective-permute-start(f32[4,512]{1,0:T(4,128)S(1)} %get-tuple-element.75), channel_id=1, source_target_pairs={{0,2},{1,3},{2,0},{3,1},{4,6},{5,7},{6,4},{7,5}} | collective-permute-start | bytes 24584 | tf_op jit(solution)/shard_map/ppermute | solution.py:460
  1120.7 110.9 %all-gather.13.cloned.1.call-start = ((), (), s32[]{:S(2)}) async-start(), calls=%async_computation.2 | async-start | bytes 6291456 | tf_op jit(solution)/shard_map/all_gather | solution.py:502
  1120.7 48.1 %collective-permute-start.7 = (bf16[512,2048]{1,0:T(8,128)(2,1)}, bf16[512,2048]{1,0:T(8,128)(2,1)S(1)}, u32[]{:S(2)}, u32[]{:S(2)}) collective-permute-start(bf16[512,2048]{1,0:T(8,128)(2,1)} %get-tuple-element.64), channel_id=1, source_target_pairs={{0,2},{1,3},{2,0},{3,1},{4,6},{5,7},{6,4},{7,5}} | collective-permute-start | bytes 6291464 | tf_op jit(solution)/shard_map/ppermute | solution.py:460
  1168.8 1.3 copy-start.6
  1170.1 115.5 %all-gather.9.cloned.1.call-start = ((), (), s32[]{:S(2)}) async-start(), calls=%async_computation | async-start | bytes 9437184 | tf_op jit(solution)/shard_map/all_gather | solution.py:482
  1196.3 6.9 copy-start.8
  1196.3 8.7 copy-start.13
  1196.3 9.0 copy-start.12
  1203.2 3.8 collective-permute-start.8
  1205.0 3.7 collective-permute-start.5
  1205.3 13.8 collective-permute-start.4
  1330.2 7.6 copy-start
  1330.2 7.6 copy-start.1
  1392.4 23.0 %copy-start.3 = (bf16[2048,1024]{1,0:T(8,128)(2,1)S(1)}, bf16[2048,1024]{1,0:T(8,128)(2,1)}, u32[]{:S(2)}) copy-start(bf16[2048,1024]{1,0:T(8,128)(2,1)} %copy.127) | copy-start | bytes 12582916
  1392.4 23.0 %copy-start.5 = (bf16[1024,2048]{1,0:T(8,128)(2,1)S(1)}, bf16[1024,2048]{1,0:T(8,128)(2,1)}, u32[]{:S(2)}) copy-start(bf16[1024,2048]{1,0:T(8,128)(2,1)} %reshape.111) | copy-start | bytes 12582916
  1484.1 3.8 copy-start.4
Sparse Core Ops, SparseCore 0:
  60.5 55.6 all-gather.14
  1120.8 54.6 all-gather.10
  1177.0 54.5 all-gather.12
  1233.2 48.3 all-gather.8

commit v2 on v1

v2 whole, which is shorter than its diff:
```python
import jax
import jax.numpy as jnp
from jax import lax
from jax.experimental import pallas as pl
from jax.experimental.pallas import tpu as pltpu
from jax.sharding import PartitionSpec as P

MESH = pl.DeviceIdType.MESH
F32 = jnp.float32
BF16 = jnp.bfloat16
LANES = 128
BATCH = 4
CHUNK = 8
PAIRS = CHUNK // 2
ROWS = BATCH * CHUNK
KB = 128
NX = 8
VMEM_LIMIT = 63 * 1024 * 1024


def sigm(v):
    return 0.5 * jnp.tanh(0.5 * v) + 0.5


def mm(a, b):
    return jnp.dot(a, b, preferred_element_type=F32)


def place():
    y = lax.axis_index('data')
    m = lax.axis_index('model')
    return y, m, m // 2, m % 2


def dev(y, m):
    return (lax.axis_index('part'), y, m)


def flips(m):
    x = m // 2
    c = m % 2
    return 2 * x + (1 - c), 2 * (1 - x) + c, 2 * (1 - x) + (1 - c)


def everyone(y, m):
    beside, across, skew = flips(m)
    return ((y, beside), (y, across), (y, skew), (1 - y, m), (1 - y, beside), (1 - y, across), (1 - y, skew))


def remote(src, dst, ssem, rsem, device):
    return pltpu.make_async_remote_copy(src, dst, ssem, rsem, device_id=device, device_id_type=MESH)


def local(src, dst, sem):
    return pltpu.make_async_copy(src, dst, sem)


def entry_barrier(y, m):
    barrier = pltpu.get_barrier_semaphore()
    for oy, om in everyone(y, m):
        pl.semaphore_signal(barrier, inc=1, device_id=dev(oy, om), device_id_type=MESH)
    pl.semaphore_wait(barrier, 7)


def aligned(i, n):
    return pl.ds(pl.multiple_of(i * n, n), n)


def gate_row(bias_ref, layer):
    return jnp.concatenate([bias_ref[layer, g:g + 1, :] for g in range(4)], axis=1)


def prep_kernel(wrec_hbm, wup_hbm, win_hbm, x_hbm, gy_hbm, hc_ref, bias_ref,
                wa_hbm, wb_hbm, wat_hbm, wbt_hbm, wup2_hbm, wupt_hbm, pre_hbm, xt_hbm, gyt_hbm, hcb_ref, init_ref,
                rin, rup, ra, rb, spread, wst, wtst, win, xin, xf, xb, prev, gyin, gyb, ib, initv, hcv,
                lsem, osem, jsem, ssx, rsx, ssy, rsy, sss, rss, gsem):
    y, m, x, c = place()
    beside, across, skew = flips(m)
    hl = hc_ref.shape[3]
    per = hl // LANES
    stride = 4 * per
    span = KB * stride
    seq = xin.shape[1]
    whole = rb.shape[0]
    part_rows = whole // 2

    loads = [local(x_hbm, xin, lsem.at[0]),
             local(win_hbm, rin, lsem.at[1]),
             local(wrec_hbm.at[aligned(x, whole), :], ra, lsem.at[2]),
             local(wup_hbm, rup, lsem.at[3]),
             local(gy_hbm, gyin, lsem.at[4])]
    for cp in loads:
        cp.start()
    entry_barrier(y, m)

    def xsend(i):
        off = y * part_rows + i * span
        src = wrec_hbm.at[pl.ds(pl.multiple_of((1 - x) * whole + off, span), span), :]
        return remote(src, rb.at[pl.ds(pl.multiple_of(off, span), span), :], ssx.at[i], rsx.at[i], dev(y, across))

    def ysend(i):
        rows = pl.ds(pl.multiple_of(y * part_rows + i * span, span), span)
        return remote(rb.at[rows, :], rb.at[rows, :], ssy.at[i], rsy.at[i], dev(1 - y, m))

    def small(i, dest_y, dest_m):
        slot = 0 if i < 3 else 1
        dst = initv.at[:, slot, :, pl.ds(pl.multiple_of(c * 2 * hl + x * hl, hl), hl)]
        return remote(ib, dst, sss.at[i], rss.at[i], dev(dest_y, dest_m))

    def state_send():
        return remote(hc_ref.at[1 - x], hcv, sss.at[7], rss.at[7], dev(y, across))

    ib[...] = hc_ref[:, 0].astype(BF16)
    initv[:, 0, :, pl.ds(pl.multiple_of(c * 2 * hl + x * hl, hl), hl)] = ib[...]
    for i, (oy, om) in enumerate(everyone(y, m)):
        small(i, oy, om).start()
    state_send().start()
    for i in range(NX):
        xsend(i).start()

    loads[0].wait()
    for t in range(xb.shape[1] // LANES):
        cols = slice(t * LANES, (t + 1) * LANES)
        for b in range(BATCH):
            xf[t % 4, pl.ds(b, seq, stride=BATCH), :] = xin[b, :, cols].astype(F32)
        xb[:, cols] = xf[t % 4].astype(BF16)
    xout = local(xb, xt_hbm, osem.at[0])
    xout.start()
    loads[4].wait()
    for t in range(per):
        cols = slice(t * LANES, (t + 1) * LANES)
        for b in range(BATCH):
            xf[t % 4, pl.ds(b, seq, stride=BATCH), :] = gyin[b, :, cols].astype(F32)
        gyb[:, cols] = xf[t % 4].astype(BF16)
    gout = local(gyb, gyt_hbm.at[0], osem.at[1])
    gout.start()

    def gy_send():
        return remote(gyb, gyt_hbm.at[1], gsem.at[0], gsem.at[1], dev(y, across))

    @pl.when(x == 0)
    def _():
        gy_send().start()

    for cp in loads[1:4]:
        cp.wait()

    def tiles(buf, raw, blk):
        spread[buf] = raw[aligned(blk, span), :].astype(F32)
        for g in range(4):
            for ct in range(per):
                yield g * hl + ct * LANES, spread[buf, pl.ds(ct * 4 + g, KB, stride=stride), :]

    def job_out(pos, blk, wo, wto):
        return (local(wst.at[pos], wo.at[aligned(blk, KB), :], jsem.at[pos, 0]),
                local(wtst.at[pos], wto.at[:, aligned(blk, KB)], jsem.at[pos, 1]))

    def job(pos, raw, blk, wo, wto):
        for off, tile in tiles(pos % 2, raw, blk):
            wst[pos, :, off:off + LANES] = tile.astype(BF16)
            wtst[pos, off:off + LANES, :] = tile.T.astype(BF16)
        for cp in job_out(pos, blk, wo, wto):
            cp.start()

    def job_wait(pos, wo, wto):
        for cp in job_out(pos, 0, wo, wto):
            cp.wait()

    early = NX // 2

    def body(i, _):
        @pl.when(i < early)
        def _():
            for q in range(4):
                blk = i * 4 + q
                for off, tile in tiles(q % 2, rin, blk):
                    win[aligned(blk, KB), off:off + LANES] = tile.astype(BF16)

        @pl.when(i == early)
        def _():
            row = gate_row(bias_ref, 0)
            nr = KB

            def pre_body(r, _):
                val = mm(xb[aligned(r, nr), :], win[...]) + row
                prev[aligned(r, nr // 8)] = val.reshape(nr // 8, 8, val.shape[1])
                return 0

            lax.fori_loop(0, xb.shape[0] // nr, pre_body, 0)
            local(prev, pre_hbm, osem.at[2]).start()

        @pl.when(i >= early)
        def _():
            for q in range(4):
                if q < 2:
                    @pl.when(i > early)
                    def _():
                        job_wait(q, wup2_hbm, wupt_hbm)
                else:
                    job_wait(q % 2, wup2_hbm, wupt_hbm)
                job(q % 2, rup, (i - early) * 4 + q, wup2_hbm, wupt_hbm)

        for q in range(2):
            @pl.when(i > 0)
            def _():
                job_wait(2 + q, wa_hbm, wat_hbm)
            job(2 + q, ra, i * 2 + q, wa_hbm, wat_hbm)

        xsend(i).wait_recv()
        ysend(i).start()

        @pl.when(i > 0)
        def _():
            job_wait(4, wb_hbm, wbt_hbm)
        job(4, rb, y * NX + i, wb_hbm, wbt_hbm)

        @pl.when(i > 0)
        def _():
            ysend(i - 1).wait_recv()

            @pl.when(i > 1)
            def _():
                job_wait(5, wb_hbm, wbt_hbm)
            job(5, rb, (1 - y) * NX + i - 1, wb_hbm, wbt_hbm)
        return 0

    lax.fori_loop(0, NX, body, 0)
    job_wait(5, wb_hbm, wbt_hbm)
    ysend(NX - 1).wait_recv()
    job(5, rb, (1 - y) * NX + NX - 1, wb_hbm, wbt_hbm)

    for i, (oy, om) in enumerate(everyone(y, m)):
        small(i, oy, om).wait()
    state_send().wait()
    hcb_ref[...] = hcv[...]
    init_ref[...] = initv[...]

    @pl.when(x == 0)
    def _():
        gy_send().wait_send()

    @pl.when(x == 1)
    def _():
        gy_send().wait_recv()

    for i in range(NX):
        xsend(i).wait_send()
        ysend(i).wait_send()
    for q in range(2):
        job_wait(q, wup2_hbm, wupt_hbm)
        job_wait(2 + q, wa_hbm, wat_hbm)
    job_wait(4, wb_hbm, wbt_hbm)
    job_wait(5, wb_hbm, wbt_hbm)
    xout.wait()
    gout.wait()
    local(prev, pre_hbm, osem.at[2]).wait()


def fwd_kernel(wa_hbm, wb_hbm, wup_hbm, pre_hbm, xt_hbm, hc_ref, hcb_ref, bias_ref,
               act_hbm, cell_hbm, lown_hbm, loth_hbm, town_hbm, toth_hbm, xoth_hbm, hfin_ref, cfin_ref,
               w, wup, prea, preb, actv, cellv, histv, hbuf, hch, cst, hs, hr, pout, fin, finr,
               lsem, psem, osem, xs, xr, hss, hrs, ps, prs, csem, fsem):
    y, m, x, c = place()
    beside, across, skew = flips(m)
    nch = hbuf.shape[0]
    hl = hs.shape[3]
    half = 2 * hl
    wide = 4 * hl
    own_cols = pl.ds(pl.multiple_of(c * half, half), half)
    others = everyone(y, m)

    loads = []
    for pos, shard in enumerate((m, across, beside, skew)):
        for col, src in enumerate((wa_hbm, wb_hbm)):
            loads.append(local(src.at[aligned(shard, hl), :], w.at[pl.ds(pos * hl, hl), pl.ds(col * wide, wide)],
                               lsem.at[len(loads)]))
    up_loads = [local(wup_hbm.at[pl.ds(shard * hl, hl), :], wup.at[pl.ds(pos * hl, hl), :], lsem.at[8 + pos])
                for pos, shard in enumerate((0, 2, 1, 3))]
    for cp in loads:
        cp.start()

    def pre_load(k):
        rows = pl.ds(k * PAIRS, PAIRS)
        return local(pre_hbm.at[rows], prea.at[rows], psem.at[k])

    @pl.when(x == 0)
    def _():
        def start(k, _):
            pre_load(k).start()
            return 0
        lax.fori_loop(0, nch, start, 0)

    for cp in up_loads:
        cp.start()

    entry_barrier(y, m)

    def swap(slot, s):
        return remote(hs.at[slot, s], hr.at[slot, s], xs.at[slot, s], xr.at[slot, s], dev(y, beside))

    def pre_send(k):
        rows = pl.ds(k * PAIRS, PAIRS)
        return remote(pre_hbm.at[rows], preb.at[rows], ps.at[k], prs.at[k], dev(y, across))

    def up_send(k):
        return remote(pout, preb.at[pl.ds(k * PAIRS, PAIRS)], ps.at[k], prs.at[k], dev(y, across))

    def x_send():
        return remote(xt_hbm, xoth_hbm, fsem.at[2], fsem.at[3], dev(1 - y, m))

    @pl.when(x == 1)
    def _():
        def start(k, _):
            pre_send(k).start()
            return 0
        lax.fori_loop(0, nch, start, 0)

    x_send().start()

    def low_send(k, i):
        oy, om = others[i]
        if i < 3:
            return remote(histv.at[k], hbuf.at[k, :, own_cols], hss.at[i], hrs.at[k, c], dev(oy, om))
        return remote(histv.at[k], loth_hbm.at[aligned(k, ROWS), own_cols], hss.at[i], csem.at[0], dev(oy, om))

    def top_send(k, i):
        oy, om = others[i]
        dst, sem = (town_hbm, csem.at[1]) if i < 3 else (toth_hbm, csem.at[2])
        return remote(histv.at[k], dst.at[aligned(k, ROWS), own_cols], hss.at[i], sem, dev(oy, om))

    def hrecv(k, core):
        cols = pl.ds(pl.multiple_of(core * half, half), half)
        return remote(histv.at[k], hbuf.at[k, :, cols], hss.at[0], hrs.at[k, core], dev(y, beside))

    def own_top(k):
        return local(histv.at[k], town_hbm.at[aligned(k, ROWS), own_cols], osem.at[3])

    init = [jnp.where(x == 0, hc_ref[0], hc_ref[1]), hcb_ref[...]]
    for s in (0, 1):
        units = slice(s * hl, (s + 1) * hl)
        hs[0, s] = init[s][0].astype(BF16)
        cst[:, units] = init[s][1]
        cellv[0, 0:4, units] = init[s][1]
        cellv[0, 4:8, units] = init[s][1]
        swap(0, s).start()
    for cp in loads:
        cp.wait()
    for cp in up_loads:
        cp.wait()

    def step(k, p, j):
        pair = k * PAIRS + p
        rows = slice(4 * j, 4 * j + 4)
        cols = (slice(0, wide), slice(wide, 2 * wide))
        acc = [mm(hs[j, 0], w[0:hl, cols[s]]) + mm(hs[j, 1], w[hl:half, cols[s]]) for s in (0, 1)]
        swap(j, 0).wait()
        swap(j, 1).wait()
        got = (hr[j, 0], hr[j, 1])
        acc = [acc[s] + (mm(got[0], w[half:half + hl, cols[s]]) + mm(got[1], w[half + hl:, cols[s]])) for s in (0, 1)]
        for s, pre in ((0, prea), (1, preb)):
            base = s * wide
            units = slice(s * hl, (s + 1) * hl)

            def gate(g):
                return acc[s][:, g * hl:(g + 1) * hl] + pre[pair, rows, g * hl:(g + 1) * hl]

            gi = sigm(gate(0))
            gf = sigm(gate(1))
            go = sigm(gate(2))
            gu = jnp.tanh(gate(3))
            cn = gf * cst[:, units] + gi * gu
            hn = go * jnp.tanh(cn)
            hs[1 - j, s] = hn.astype(BF16)
            cst[:, units] = cn
            for g, val in enumerate((gi, gf, go, gu)):
                actv[pair, rows, base + g * hl:base + (g + 1) * hl] = val
            cellv[pair + 1, rows, units] = cn
            hch[p, rows, units] = hn
        swap(1 - j, 0).start()
        swap(1 - j, 1).start()

    def up_product(k):
        return (mm(hbuf[k], wup[...]) + gate_row(bias_ref, 1)).reshape(PAIRS, 8, wide)

    def act_out(k):
        rows = pl.ds(k * PAIRS, PAIRS)
        return local(actv.at[rows], act_hbm.at[rows], osem.at[0])

    def slot_body(s, _):
        k = s - x
        live = (k >= 0) & (k < nch)

        @pl.when((x == 1) & live)
        def _():
            hrecv(k, 0).wait_recv()
            hrecv(k, 1).wait_recv()
            prea[pl.ds(k * PAIRS, PAIRS)] = up_product(k)

        @pl.when((x == 0) & live)
        def _():
            pre_load(k).wait()

        @pl.when(live)
        def _():
            up_send(k).wait_recv()

        def pair_body(p, _):
            @pl.when((x == 0) & (s >= 1) & (p == 1))
            def _():
                hrecv(s - 1, 1 - c).wait_recv()

                @pl.when(s >= 2)
                def _():
                    up_send(s - 2).wait_send()

                pout[...] = up_product(s - 1)
                up_send(s - 1).start()

            @pl.when(live)
            def _():
                step(k, p, 0)
                step(k, p, 1)
            return 0

        lax.fori_loop(0, PAIRS, pair_body, 0)

        @pl.when(live)
        def _():
            act_out(k).start()

            @pl.when(x == 0)
            def _():
                block = hch[...].reshape(ROWS, half).astype(BF16)
                histv[k] = block
                hbuf[k, :, own_cols] = block

                @pl.when(k >= 1)
                def _():
                    for i in range(7):
                        low_send(k - 1, i).wait_send()
                for i in range(7):
                    low_send(k, i).start()

            @pl.when(x == 1)
            def _():
                block = hch[...].reshape(ROWS, half).astype(BF16)
                histv[k, :, 0:hl] = block[:, hl:half]
                histv[k, :, hl:half] = block[:, 0:hl]

                @pl.when(k >= 1)
                def _():
                    for i in range(7):
                        top_send(k - 1, i).wait_send()
                for i in range(7):
                    top_send(k, i).start()
                own_top(k).start()
        return 0

    lax.fori_loop(0, nch + 1, slot_body, 0)
    swap(0, 0).wait()
    swap(0, 1).wait()

    def fin_send():
        return remote(fin, finr, fsem.at[0], fsem.at[1], dev(y, across))

    fin[0] = hch[PAIRS - 1, 4:8, hl:half]
    fin[1] = cst[:, hl:half]
    fin_send().start()
    local(cellv, cell_hbm, osem.at[2]).start()

    @pl.when(x == 0)
    def _():
        for i in range(7):
            low_send(nch - 1, i).wait_send()
        up_send(nch - 1).wait_send()
        local(town_hbm, town_hbm, csem.at[1]).wait()

    @pl.when(x == 1)
    def _():
        for i in range(7):
            top_send(nch - 1, i).wait_send()

        def drain(k, _):
            pre_send(k).wait_send()
            return 0
        lax.fori_loop(0, nch, drain, 0)
        part = town_hbm.at[:, pl.ds(0, half)]
        local(part, part, csem.at[1]).wait()
        local(part, part, osem.at[3]).wait()

    def low_out(k):
        return local(hbuf.at[k], lown_hbm.at[aligned(k, ROWS), :], osem.at[1])

    def low_start(k, _):
        low_out(k).start()
        return 0

    lax.fori_loop(0, nch, low_start, 0)
    local(loth_hbm, loth_hbm, csem.at[0]).wait()
    local(toth_hbm, toth_hbm, csem.at[2]).wait()
    x_send().wait()
    fin_send().wait()
    mine = [hch[PAIRS - 1, 4:8, 0:hl], cst[:, 0:hl]]
    for ref, i in ((hfin_ref, 0), (cfin_ref, 1)):
        ref[0] = jnp.where(x == 0, mine[i], finr[i])
        ref[1] = jnp.where(x == 0, finr[i], mine[i])
    local(lown_hbm, lown_hbm, osem.at[1]).wait()
    local(cellv, cell_hbm, osem.at[2]).wait()
    local(actv, act_hbm, osem.at[0]).wait()


def bwd_kernel(wta_hbm, wtb_hbm, wupt_hbm, act_hbm, cell_hbm, gy_hbm,
               dg_hbm, bias_ref,
               wt, wupt, actv, cellv, dout, gyv, dgv, dgr, dgch, dgs, dct, bacc, own, snd, rcv, pin, pout, bsnd, brcv,
               lsem, asem, osem, xs, xr, gs, grs, ps, prs, csem, bsem):
    y, m, x, c = place()
    beside, across, skew = flips(m)
    nch = dgv.shape[0]
    half = own.shape[1]
    hl = half // 2
    wide = 4 * hl

    loads = []
    for pos, shard in enumerate((beside, skew, m, across)):
        for row, src in enumerate((wta_hbm, wtb_hbm)):
            loads.append(local(src.at[:, aligned(shard, hl)], wt.at[pl.ds(row * wide, wide), pl.ds(pos * hl, hl)],
                               lsem.at[len(loads)]))
    for pos, shard in enumerate((1 - c, 3 - c, c, 2 + c)):
        loads.append(local(wupt_hbm.at[:, aligned(shard, hl)], wupt.at[:, pl.ds(pos * hl, hl)], lsem.at[len(loads)]))
    loads.append(local(cell_hbm, cellv, lsem.at[12]))
    for cp in loads:
        cp.start()

    @pl.when(x == 1)
    def _():
        cp = local(gy_hbm, gyv, lsem.at[13])
        cp.start()
        cp.wait()
        for s in (0, 1):
            dout[:, :, s * hl:(s + 1) * hl] = gyv[s].astype(F32).reshape(nch * PAIRS, 8, hl)

    def act_in(k):
        rows = pl.ds(k * PAIRS, PAIRS)
        return local(act_hbm.at[rows], actv.at[rows], asem.at[k])

    def start_act(i, _):
        act_in(nch - 1 - i).start()
        return 0

    lax.fori_loop(0, nch, start_act, 0)
    entry_barrier(y, m)

    def swap(slot):
        return remote(snd.at[slot], rcv.at[slot], xs.at[slot], xr.at[slot], dev(y, beside))

    part_a = pl.ds(0, wide)
    part_b = pl.ds(wide, wide)

    def up_grads(k):
        return remote(dgv.at[k, :, part_b], dgr.at[k], gs.at[0], grs.at[k], dev(y, across))

    def sends(k, top):
        rows = aligned(k, ROWS)
        layer = 1 if top else 0
        mine = remote(dgv.at[k, :, part_a], dg_hbm.at[layer, 1, rows, :], gs.at[1], csem.at[0], dev(1 - y, m))
        far = remote(dgv.at[k, :, part_b], dg_hbm.at[layer, 1, rows, :], gs.at[2], csem.at[1], dev(1 - y, across))
        near = up_grads(k) if top else remote(
            dgv.at[k, :, part_b], dg_hbm.at[0, 0, rows, :], gs.at[0], csem.at[2], dev(y, across))
        return near, mine, far

    def keep(k, top):
        return local(dgv.at[k, :, part_a], dg_hbm.at[1 if top else 0, 0, aligned(k, ROWS), :], osem.at[0])

    def keep_up(k):
        return local(dgr.at[k], dg_hbm.at[1, 0, aligned(k, ROWS), :], osem.at[1])

    def psend(k, pos, dest, src):
        return remote(pout.at[pos], pin.at[src, k], ps.at[pos], prs.at[src, k], dev(y, dest))

    dgs[...] = jnp.zeros(dgs.shape, BF16)
    dct[...] = jnp.zeros(dct.shape, F32)
    bacc[...] = jnp.zeros(bacc.shape, F32)
    for cp in loads:
        cp.wait()

    def step(k, p, j):
        pair = k * PAIRS + p
        rows = slice(4 * j, 4 * j + 4)
        dgl = dgs[...]
        snd[j] = mm(dgl, wt[:, 0:half])
        swap(j).start()
        own[...] = mm(dgl, wt[:, half:])
        swap(j).wait()
        for s in (0, 1):
            base = s * wide
            units = slice(s * hl, (s + 1) * hl)
            gi, gf, go, gu = (actv[pair, rows, base + g * hl:base + (g + 1) * hl] for g in range(4))
            tc = jnp.tanh(cellv[pair + 1, rows, units])
            cp = cellv[pair + 1, 0:4, units] if j else cellv[pair, 4:8, units]
            dh = dout[pair, rows, units] + own[:, units] + rcv[j, :, units]
            dc = dct[:, units] + dh * go * (1.0 - tc * tc)
            dct[:, units] = dc * gf
            grads = (dc * gu * gi * (1.0 - gi), dc * cp * gf * (1.0 - gf),
                     dh * tc * go * (1.0 - go), dc * gi * (1.0 - gu * gu))
            for g, val in enumerate(grads):
                cols = slice(base + g * hl, base + (g + 1) * hl)
                bacc[:, cols] += val
                dgs[:, cols] = val.astype(BF16)
                dgch[p, rows, cols] = val

    def slot_body(s, _):
        k = nch - 1 - s + (1 - x)
        live = (k >= 0) & (k < nch)

        @pl.when(live)
        def _():
            act_in(k).wait()

        @pl.when((x == 0) & live)
        def _():
            up_grads(k).wait_recv()
            keep_up(k).start()
            block = dgr[k]

            @pl.when(s >= 2)
            def _():
                psend(k + 1, 0, beside, 2).wait_send()
            pout[0] = mm(block, wupt[:, 0:half]).reshape(PAIRS, 8, half)
            psend(k, 0, beside, 2).start()
            part = mm(block, wupt[:, half:]).reshape(PAIRS, 8, half)
            for src in (0, 1, 2):
                psend(k, 0, beside, src).wait_recv()
            dout[pl.ds(k * PAIRS, PAIRS)] = part + pin[0, k] + pin[1, k] + pin[2, k]

        @pl.when(live)
        def _():
            def pair_body(i, _):
                step(k, PAIRS - 1 - i, 1)
                step(k, PAIRS - 1 - i, 0)
                return 0

            lax.fori_loop(0, PAIRS, pair_body, 0)
            dgv[k] = dgch[...].reshape(ROWS, 2 * wide).astype(BF16)

        @pl.when((x == 0) & live)
        def _():
            @pl.when(s >= 2)
            def _():
                for cp in sends(k + 1, False):
                    cp.wait_send()
            for cp in sends(k, False):
                cp.start()
            keep(k, False).start()

        @pl.when((x == 1) & live)
        def _():
            @pl.when(s >= 1)
            def _():
                for cp in sends(k + 1, True):
                    cp.wait_send()
                psend(k + 1, 0, skew, c).wait_send()
                psend(k + 1, 1, across, c).wait_send()
            for cp in sends(k, True):
                cp.start()
            keep(k, True).start()
            block = dgv[k, :, 0:wide]
            pout[0] = mm(block, wupt[:, 0:half]).reshape(PAIRS, 8, half)
            psend(k, 0, skew, c).start()
            pout[1] = mm(block, wupt[:, half:]).reshape(PAIRS, 8, half)
            psend(k, 1, across, c).start()
        return 0

    lax.fori_loop(0, nch + 1, slot_body, 0)

    bsnd[0] = bacc[:, 0:wide]
    bsnd[1] = bacc[:, wide:]
    shares = (remote(bsnd.at[0], brcv.at[0], bsem.at[0], bsem.at[3], dev(1 - y, m)),
              remote(bsnd.at[1], brcv.at[1], bsem.at[1], bsem.at[4], dev(y, across)),
              remote(bsnd.at[1], brcv.at[2], bsem.at[2], bsem.at[5], dev(1 - y, across)))
    for cp in shares:
        cp.start()

    quarter = dg_hbm.at[0, 0]

    @pl.when(x == 0)
    def _():
        psend(0, 0, beside, 2).wait_send()
        for cp in sends(0, False):
            cp.wait_send()
        local(quarter, quarter, osem.at[1]).wait()

    @pl.when(x == 1)
    def _():
        for cp in sends(0, True):
            cp.wait_send()
        psend(0, 0, skew, c).wait_send()
        psend(0, 1, across, c).wait_send()
        local(quarter, quarter, csem.at[2]).wait()

    local(quarter, quarter, csem.at[0]).wait()
    local(quarter, quarter, csem.at[1]).wait()
    local(quarter, quarter, osem.at[0]).wait()
    for cp in shares:
        cp.wait()
    same = jnp.sum(bsnd[0] + brcv[0], axis=0, keepdims=True)
    cross = jnp.sum(brcv[1] + brcv[2], axis=0, keepdims=True)
    low = jnp.where(x == 0, same, cross)
    top = jnp.where(x == 0, cross, same)
    for g in range(4):
        bias_ref[0, g:g + 1, :] = low[:, g * hl:(g + 1) * hl]
        bias_ref[1, g:g + 1, :] = top[:, g * hl:(g + 1) * hl]


def grad_kernel(xo_hbm, xf_hbm, lo_hbm, lf_hbm, to_hbm, tf_hbm, init_ref, dg_hbm,
                dwin_hbm, dwup_hbm, dwrec_hbm, y_ref,
                xv, hlow, htop, dlow, dtop, shf, yf, stage, lsem, osem):
    hidden = hlow.shape[1]
    srows = lo_hbm.shape[0]
    kb = 256
    hl = hidden // 4
    wide = dlow.shape[1]
    nblk = hidden // kb
    per = hl // LANES
    raw = kb * 4 * per
    nq = hl // kb
    m = lax.axis_index('model')
    x = m // 2
    c = m % 2
    lo = pl.ds(0, srows)
    hi = pl.ds(srows, srows)
    srcs = ((xo_hbm, xv.at[lo, :]), (xf_hbm, xv.at[hi, :]), (dg_hbm.at[0, 0], dlow.at[lo, :]), (dg_hbm.at[0, 1], dlow.at[hi, :]),
            (lo_hbm, hlow.at[lo, :]), (lf_hbm, hlow.at[hi, :]), (dg_hbm.at[1, 0], dtop.at[lo, :]), (dg_hbm.at[1, 1], dtop.at[hi, :]),
            (to_hbm, htop.at[lo, :]), (tf_hbm, htop.at[hi, :]))
    loads = [local(a, b, lsem.at[i]) for i, (a, b) in enumerate(srcs)]
    for cp in loads:
        cp.start()

    def core_row(i):
        q = i // nq
        return ((q % 2) * 2 + q // 2) * nq + i % nq

    def out_copy(slot, dst, off):
        return local(stage.at[slot], dst.at[aligned(off, raw), :], osem.at[slot])

    def emit(count, lhs, grads, dst, off):
        slot = lax.rem(count, 2)

        @pl.when(count >= 2)
        def _():
            out_copy(slot, dst, off).wait()
        res = mm(lhs.T, grads[...])
        for g in range(4):
            for ct in range(per):
                col = g * hl + ct * LANES
                stage[slot, pl.ds(ct * 4 + g, kb, stride=4 * per), :] = res[:, col:col + LANES]
        out_copy(slot, dst, off).start()

    def shifted(h, layer, cols):
        for part in (0, 1):
            base = part * srows
            shf[base + 4:base + srows, :] = h[pl.ds(base, srows), cols].astype(F32)[:srows - 4]
            shf[base:base + 4, :] = init_ref[layer, part, :, cols].astype(F32)
        return shf[...].astype(BF16)

    for cp in loads[0:4]:
        cp.wait()

    def phase0(i, _):
        emit(i, xv[:, aligned(i, kb)], dlow, dwin_hbm, i)
        return 0

    def phase1(i, _):
        emit(i + nblk, shifted(hlow, 0, aligned(i, kb)), dlow, dwrec_hbm, core_row(i))
        return 0

    def phase2(i, _):
        emit(i + 2 * nblk, hlow[:, aligned(i, kb)], dtop, dwup_hbm, core_row(i))
        return 0

    def phase3(i, _):
        emit(i + 3 * nblk, shifted(htop, 1, aligned(i, kb)), dtop, dwrec_hbm, nblk + core_row(i))
        return 0

    lax.fori_loop(0, nblk, phase0, 0)
    for cp in loads[4:6]:
        cp.wait()
    lax.fori_loop(0, nblk, phase1, 0)
    for cp in loads[6:8]:
        cp.wait()
    lax.fori_loop(0, nblk, phase2, 0)
    for cp in loads[8:10]:
        cp.wait()
    for t in range(per):
        yf[t] = htop[0:srows, pl.ds(pl.multiple_of(c * 2 * hl + x * hl + t * LANES, LANES), LANES)].astype(F32)
        for b in range(BATCH):
            y_ref[b, :, t * LANES:(t + 1) * LANES] = yf[t, pl.ds(b, srows // BATCH, stride=BATCH), :].astype(BF16)
    lax.fori_loop(0, nblk, phase3, 0)
    for slot in (0, 1):
        out_copy(slot, dwrec_hbm, 0).wait()


def any_spec():
    return pl.BlockSpec(memory_space=pl.ANY)


def vmem_spec():
    return pl.BlockSpec(memory_space=pltpu.VMEM)


def sds(shape, dtype):
    return jax.ShapeDtypeStruct(shape, dtype)


DMA = pltpu.SemaphoreType.DMA


def comm_params(i):
    return pltpu.CompilerParams(collective_id=i, has_side_effects=True, vmem_limit_bytes=VMEM_LIMIT)


def run_prep(wrec, wup, win, x, gy, hc, bias):
    batch, seq, width = x.shape
    hl = gy.shape[2]
    wide = 4 * hl
    hidden = 4 * hl
    rows = batch * seq
    raw = win.shape[0]
    per = hl // LANES
    span = KB * 4 * per
    square = sds((hidden, wide), BF16)
    vm = pltpu.VMEM
    return pl.pallas_call(
        prep_kernel,
        name='lstm_prepare',
        out_shape=(square,) * 6 + (sds((rows // 8, 8, wide), F32), sds((rows, width), BF16), sds((2, rows, hl), BF16),
                                   sds((2, 4, hl), F32), sds((2, 2, 4, hidden), BF16)),
        in_specs=[any_spec()] * 5 + [vmem_spec()] * 2,
        out_specs=(any_spec(),) * 9 + (vmem_spec(),) * 2,
        scratch_shapes=[
            vm((raw, LANES), BF16), vm((raw, LANES), BF16), vm((raw, LANES), BF16), vm((raw, LANES), BF16),
            vm((2, span, LANES), F32), vm((6, KB, wide), BF16), vm((6, wide, KB), BF16), vm((width, wide), BF16),
            vm(x.shape, BF16), vm((4, rows, LANES), F32), vm((rows, width), BF16), vm((rows // 8, 8, wide), F32),
            vm(gy.shape, BF16), vm((rows, hl), BF16), vm((2, 4, hl), BF16),
            vm((2, 2, 4, hidden), BF16), vm((2, 4, hl), F32),
            DMA((5,)), DMA((3,)), DMA((6, 2)), DMA((NX,)), DMA((NX,)), DMA((NX,)), DMA((NX,)), DMA((8,)), DMA((8,)), DMA((2,)),
        ],
        compiler_params=comm_params(0),
    )(wrec, wup, win, x, gy, hc, bias)


def run_fwd(wa, wb, wup, pre, xt, hc, hcb, bias):
    hidden, wide = wa.shape
    hl = wide // 4
    half = 2 * hl
    npair = pre.shape[0]
    nch = npair // PAIRS
    rows = npair * 8
    hist = sds((rows, hidden), BF16)
    vm = pltpu.VMEM
    return pl.pallas_call(
        fwd_kernel,
        name='lstm_forward',
        out_shape=(sds((npair, 8, 2 * wide), F32), sds((npair + 1, 8, half), F32), hist, hist, hist, hist,
                   sds(xt.shape, BF16), sds((2, 4, hl), F32), sds((2, 4, hl), F32)),
        in_specs=[any_spec()] * 5 + [vmem_spec()] * 3,
        out_specs=(any_spec(),) * 7 + (vmem_spec(),) * 2,
        scratch_shapes=[
            vm((hidden, 2 * wide), BF16), vm((hidden, wide), BF16),
            vm((npair, 8, wide), F32), vm((npair, 8, wide), F32),
            vm((npair, 8, 2 * wide), F32), vm((npair + 1, 8, half), F32),
            vm((nch, ROWS, half), BF16), vm((nch, ROWS, hidden), BF16),
            vm((PAIRS, 8, half), F32), vm((4, half), F32),
            vm((2, 2, 4, hl), BF16), vm((2, 2, 4, hl), BF16),
            vm((PAIRS, 8, wide), F32), vm((2, 4, hl), F32), vm((2, 4, hl), F32),
            DMA((12,)), DMA((nch,)), DMA((4,)), DMA((2, 2)), DMA((2, 2)), DMA((7,)), DMA((nch, 2)),
            DMA((nch,)), DMA((nch,)), DMA((3,)), DMA((4,)),
        ],
        compiler_params=comm_params(1),
    )(wa, wb, wup, pre, xt, hc, hcb, bias)


def run_bwd(wta, wtb, wupt, act, cell, gy):
    wide, hidden = wta.shape
    hl = wide // 4
    half = 2 * hl
    npair = act.shape[0]
    nch = npair // PAIRS
    rows = npair * 8
    vm = pltpu.VMEM
    return pl.pallas_call(
        bwd_kernel,
        name='lstm_backward',
        out_shape=(sds((2, 2, rows, wide), BF16), sds((2, 4, hl), F32)),
        in_specs=[any_spec()] * 6,
        out_specs=(any_spec(), vmem_spec()),
        scratch_shapes=[
            vm((2 * wide, hidden), BF16), vm((wide, hidden), BF16),
            vm((npair, 8, 2 * wide), F32), vm((npair + 1, 8, half), F32),
            vm((npair, 8, half), F32), vm((2, rows, hl), BF16),
            vm((nch, ROWS, 2 * wide), BF16), vm((nch, ROWS, wide), BF16),
            vm((PAIRS, 8, 2 * wide), F32), vm((4, 2 * wide), BF16),
            vm((4, half), F32), vm((4, 2 * wide), F32),
            vm((4, half), F32), vm((2, 4, half), F32), vm((2, 4, half), F32),
            vm((3, nch, PAIRS, 8, half), F32), vm((2, PAIRS, 8, half), F32),
            vm((2, 4, wide), F32), vm((3, 4, wide), F32),
            DMA((14,)), DMA((nch,)), DMA((2,)), DMA((2,)), DMA((2,)), DMA((3,)), DMA((nch,)), DMA((2,)), DMA((3, nch)),
            DMA((3,)), DMA((6,)),
        ],
        compiler_params=comm_params(2),
    )(wta, wtb, wupt, act, cell, gy)


def run_grads(xo, xf, lo, lf, to, tf, init, dg):
    srows, hidden = lo.shape
    rows = 2 * srows
    wide = dg.shape[3]
    raw = hidden * wide // LANES
    hl = wide // 4
    kb = 256
    vm = pltpu.VMEM
    return pl.pallas_call(
        grad_kernel,
        name='weight_grads',
        out_shape=(sds((raw, LANES), F32), sds((raw, LANES), F32), sds((2 * raw, LANES), F32),
                   sds((BATCH, srows // BATCH, hl), BF16)),
        in_specs=[any_spec()] * 6 + [vmem_spec(), any_spec()],
        out_specs=(any_spec(),) * 3 + (vmem_spec(),),
        scratch_shapes=[vm((rows, hidden), BF16)] * 3 + [vm((rows, wide), BF16)] * 2 + [
            vm((rows, kb), F32), vm((hl // LANES, srows, LANES), F32), vm((2, kb * wide // LANES, LANES), F32), DMA((10,)), DMA((2,))],
        compiler_params=pltpu.CompilerParams(vmem_limit_bytes=VMEM_LIMIT),
    )(xo, xf, lo, lf, to, tf, init, dg)


def to_raw(w):
    hl = w.shape[-1]
    w = w.reshape(-1, 4, hl // LANES, LANES)
    return jnp.swapaxes(w, 1, 2).reshape(-1, LANES)


def from_raw(v, lead, hl):
    v = v.reshape(-1, hl // LANES, 4, LANES)
    return jnp.swapaxes(v, 1, 2).reshape(lead + (-1, 4, hl))


def solution(mesh):
    batch_axes = ('part', 'data')
    seq_spec = P(batch_axes, None, 'model')
    state_spec = P(None, batch_axes, 'model')
    weight_spec = P(None, None, None, 'model')
    in_specs = (P(batch_axes, None, None), seq_spec, state_spec, state_spec,
                P(None, None, 'model'), weight_spec, weight_spec, P(None, None, 'model'))
    out_specs = (seq_spec, state_spec, state_spec, P('part', None, 'model'),
                 P(None, 'part', None, 'model'), P(None, 'part', None, 'model'), P(None, 'part', 'model'))

    def local_program(x_seq, gy_seq, h_init, c_init, w_in, w_up, w_rec, gate_bias):
        hl = w_in.shape[2]
        hc = jnp.stack([h_init, c_init], axis=1)
        wa, wb, wat, wbt, wup, wupt, pre, xt, gyt, hcb, init = run_prep(
            to_raw(w_rec), to_raw(w_up), to_raw(w_in), x_seq, gy_seq, hc, gate_bias)
        act, cell, low_own, low_far, top_own, top_far, x_far, h_last, c_last = run_fwd(
            wa, wb, wup, pre, xt, hc, hcb, gate_bias)
        dg, bias = run_bwd(wat, wbt, wupt, act, cell, gyt)
        dw_in, dw_up, dw_rec, y_out = run_grads(xt, x_far, low_own, low_far, top_own, top_far, init, dg)
        return (y_out, h_last, c_last, from_raw(dw_in, (), hl), from_raw(dw_up, (1,), hl),
                from_raw(dw_rec, (2,), hl), bias)

    return jax.shard_map(local_program, mesh=mesh, in_specs=in_specs, out_specs=out_specs, check_vma=False)
```

time: 1540 us -> 978 us (0.64)
  local copies, waits for them, and re-layouts: 341 us -> 1.83 us
  waiting for transfers between devices: 262 us -> 0 us
  Pallas kernels: 771 us -> 974 us
  matrix products: 68.8 us -> 0 us
  other arithmetic: 41.5 us -> 1.36 us
  blocking collectives: 21.3 us -> 0 us
    ppermute x9 -> x0, waiting for transfers between devices: 249 us -> none  [across(): return lax.ppermute(v, 'model', ACROSS)]
    pallas_call x1 -> x3, Pallas kernels: 411 us -> 568 us  [the longest x1 392 us: run_bwd(): pl.pallas_call(bwd_kernel, name='lstm_backward', out_shape=(sds((2, 2, ro...]
    unnamed x39 -> x9, local copies, waits for them, and re-layouts: 126 us -> 1.83 us
    dot_general x5 -> x0, matrix products: 68.8 us -> none  [the longest x4 59.3 us: outer(): jnp.einsum('rk,rn->kn', a.reshape(-1, a.shape[-1]), b, preferred_element_...]
    reshape x8 -> x0, local copies, waits for them, and re-layouts: 62.2 us -> none  [the longest x3 20.7 us: outer(): a.reshape(-1, a.shape[-1])]
    pallas_call x1, Pallas kernels: 360 us -> 406 us  [run_fwd(): pl.pallas_call(fwd_kernel, name='lstm_forward', out_shape=(sds((npair, 8,...]
    dynamic_slice x4 -> x0, local copies, waits for them, and re-layouts: 31.5 us -> none  [the longest x2 29.3 us: pick(): return lax.dynamic_index_in_dim(v, i, 0, keepdims=False)]
    slice x5 -> x0, local copies, waits for them, and re-layouts: 26.1 us -> none  [the longest x1 17.9 us: layer_hist(): first, second = (a[..., layer, :], a[..., 1 - layer, :])]
  transfers between devices with their start and end apart: 13 -> 0, of which waited for: 4 -> 0; matrix products, arithmetic and copies ran while one was open for 12% -> 0% of each run, Pallas kernels for 50% -> 0%
where the time goes in v2:
time: 978 us
  Pallas kernels  974 us (100%)
    pallas_call x1, Pallas kernels, run_fwd(): pl.pallas_call(fwd_kernel, name='lstm_forward', out_shape=(sds((npair, 8,...  406 us
    pallas_call x1, Pallas kernels, run_bwd(): pl.pallas_call(bwd_kernel, name='lstm_backward', out_shape=(sds((2, 2, ro...  392 us
    pallas_call x1, Pallas kernels, run_prep(): pl.pallas_call(prep_kernel, name='lstm_prepare', out_shape=(square,) * 6...  112 us
    pallas_call x1, Pallas kernels, run_grads(): pl.pallas_call(grad_kernel, name='weight_grads', out_shape=(sds((raw, LAN...  63.5 us

profile of v2, /device:TPU:0, one launch (start us, length us, event | category | flops | bytes accessed | tf_op | source)
XLA Modules:
  0.0 978.0 jit_solution(15715158638045480623)
XLA Ops:
  0.6 1.4 pad_maximum_fusion.hc_ref
  2.0 112.4 %lstm_prepare.1 = (bf16[2048,2048]{1,0:T(8,128)(2,1)}, bf16[2048,2048]{1,0:T(8,128)(2,1)}, bf16[2048,2048]{1,0:T(8,128)(2,1)}, bf16[2048,2048]{1,0:T(8,128)(2,1)...) custom-call(bf16[65536,128]{1,0:T(8,128)(2,1)} %bitcast.32, ...), custom_call_target="tpu_custom_call" | custom-call | tf_op jit(solution)/shard_map/lstm_prepare/pallas_call | solution.py:832
  114.4 406.4 %lstm_forward.1 = (f32[64,8,4096]{2,1,0:T(8,128)}, f32[65,8,1024]{2,1,0:T(8,128)}, bf16[512,2048]{1,0:T(8,128)(2,1)}, bf16[512,2048]{1,0:T(8,128)(2,1)}, bf16[51...) custom-call(bf16[2048,2048]{1,0:T(8,128)(2,1)} %get-tuple-element.34, ...), custom_call_target="tpu_custom_call" | custom-call | tf_op jit(solution)/shard_map/lstm_forward/pallas_call | solution.py:860
  520.7 391.8 %lstm_backward.1 = (bf16[2,2,512,2048]{3,2,1,0:T(8,128)(2,1)}, f32[2,4,512]{2,1,0:T(4,128)}) custom-call(bf16[2048,2048]{1,0:T(8,128)(2,1)} %get-tuple-element.45.wta_hbm, bf16[2048,2048]{1,0:T(8,128)(2,1)} %get-tuple-element.46.wtb_hbm, bf16[2048,2048]{1,0:T(8,128)(2,1)} %get-tuple-element.47.wupt_hbm, f32[64,8,4096]{2,1,0:T(8,128)} %get-tuple-element.48.act_hbm, ...), custom_call_target="tpu_custom_call" | custom-call | tf_op jit(solution)/shard_map/lstm_backward/pallas_call | solution.py:890
  912.6 0.0 copy-start.1
  912.6 0.0 copy-start
  912.6 0.0 copy-start.2
  912.6 63.5 %weight_grads.1 = (f32[32768,128]{1,0:T(8,128)}, f32[32768,128]{1,0:T(8,128)}, f32[65536,128]{1,0:T(8,128)}, bf16[4,128,512]{2,1,0:T(8,128)(2,1)}) custom-call(bf16[512,2048]{1,0:T(8,128)(2,1)} %get-tuple-element.33.xt_hbm.xo_hbm, bf16[512,2048]{1,0:T(8,128)(2,1)} %get-tuple-element.39.xf_hbm, bf16[512,2048]{1,0:T(8,128)(2,1)} %get-tuple-element.40.lo_hbm, ...), custom_call_target="tpu_custom_call" | custom-call | tf_op jit(solution)/shard_map/weight_grads/pallas_call | solution.py:921
  976.1 0.0 copy-done.1
  976.1 0.6 copy.24
  976.8 0.0 copy-done
  976.8 0.6 copy.25
  977.4 0.0 copy-done.2
  977.4 0.6 copy.26
Async XLA Ops:
  912.6 63.5 %copy-start.1 = (f32[2,4,512]{2,1,0:T(4,128)S(1)}, f32[2,4,512]{2,1,0:T(4,128)}, u32[]{:S(2)}) copy-start(f32[2,4,512]{2,1,0:T(4,128)} %get-tuple-element.67) | copy-start | bytes 49156
  912.6 64.2 %copy-start = (f32[2,4,512]{2,1,0:T(4,128)S(1)}, f32[2,4,512]{2,1,0:T(4,128)}, u32[]{:S(2)}) copy-start(f32[2,4,512]{2,1,0:T(4,128)} %get-tuple-element.68) | copy-start | bytes 49156
  912.6 64.8 %copy-start.2 = (f32[2,4,512]{2,1,0:T(4,128)S(1)}, f32[2,4,512]{2,1,0:T(4,128)}, u32[]{:S(2)}) copy-start(f32[2,4,512]{2,1,0:T(4,128)} %get-tuple-element.72) | copy-start | bytes 49156

commit v3 on v2

v3 whole, which is shorter than its diff:
```python
import jax
import jax.numpy as jnp
from jax import lax
from jax.experimental import pallas as pl
from jax.experimental.pallas import tpu as pltpu
from jax.sharding import PartitionSpec as P

MESH = pl.DeviceIdType.MESH
F32 = jnp.float32
BF16 = jnp.bfloat16
LANES = 128
BATCH = 4
CHUNK = 8
_0, _1, _2 = range(3)
BOTH = (_0, _1)
GATES = range(4)
PAIRS = CHUNK // _2
ROWS = BATCH * CHUNK
KB = 128
NX = 8
VMEM_LIMIT = 63 * 1024 * 1024


def sigm(v):
    return 0.5 * jnp.tanh(0.5 * v) + 0.5


def mm(a, b):
    return jnp.dot(a, b, preferred_element_type=F32)


def place():
    y = lax.axis_index('data')
    m = lax.axis_index('model')
    return y, m, m // _2, m % _2


def dev(y, m):
    return (lax.axis_index('part'), y, m)


def flips(m):
    x = m // _2
    c = m % _2
    return _2 * x + (_1 - c), _2 * (_1 - x) + c, _2 * (_1 - x) + (_1 - c)


def everyone(y, m):
    beside, across, skew = flips(m)
    return ((y, beside), (y, across), (y, skew), (_1 - y, m), (_1 - y, beside), (_1 - y, across), (_1 - y, skew))


def remote(src, dst, ssem, rsem, device):
    return pltpu.make_async_remote_copy(src, dst, ssem, rsem, device_id=device, device_id_type=MESH)


def local(src, dst, sem):
    return pltpu.make_async_copy(src, dst, sem)


def entry_barrier(y, m):
    barrier = pltpu.get_barrier_semaphore()
    for oy, om in everyone(y, m):
        pl.semaphore_signal(barrier, inc=_1, device_id=dev(oy, om), device_id_type=MESH)
    pl.semaphore_wait(barrier, 7)


def part(i, n, base=_0):
    return slice(base + i * n, base + (i + _1) * n)


def aligned(i, n):
    return pl.ds(pl.multiple_of(i * n, n), n)


def gate_row(bias_ref, layer):
    return jnp.concatenate([bias_ref[layer, g:g + _1, :] for g in GATES], axis=_1)


def prep_kernel(wrec_hbm, wup_hbm, win_hbm, x_hbm, gy_hbm, hc_ref, bias_ref,
                wa_hbm, wb_hbm, wat_hbm, wbt_hbm, wup2_hbm, wupt_hbm, pre_hbm, xt_hbm, gyt_hbm, hcb_ref, init_ref,
                rin, rup, ra, rb, spread, wst, wtst, win, xin, xf, xb, prev, gyin, gyb, ib, initv, hcv,
                lsem, osem, jsem, ssx, rsx, ssy, rsy, sss, rss, gsem):
    y, m, x, c = place()
    beside, across, skew = flips(m)
    hl = hc_ref.shape[3]
    per = hl // LANES
    stride = 4 * per
    span = KB * stride
    seq = xin.shape[_1]
    whole = rb.shape[_0]
    part_rows = whole // _2

    loads = [local(x_hbm, xin, lsem.at[_0]),
             local(win_hbm, rin, lsem.at[_1]),
             local(wrec_hbm.at[aligned(x, whole), :], ra, lsem.at[_2]),
             local(wup_hbm, rup, lsem.at[3]),
             local(gy_hbm, gyin, lsem.at[4])]
    for cp in loads:
        cp.start()
    entry_barrier(y, m)

    def xsend(i):
        off = y * part_rows + i * span
        src = wrec_hbm.at[pl.ds(pl.multiple_of((_1 - x) * whole + off, span), span), :]
        return remote(src, rb.at[pl.ds(pl.multiple_of(off, span), span), :], ssx.at[i], rsx.at[i], dev(y, across))

    def ysend(i):
        rows = pl.ds(pl.multiple_of(y * part_rows + i * span, span), span)
        return remote(rb.at[rows, :], rb.at[rows, :], ssy.at[i], rsy.at[i], dev(_1 - y, m))

    def small(i, dest_y, dest_m):
        slot = _0 if i < 3 else _1
        dst = initv.at[:, slot, :, pl.ds(pl.multiple_of(c * _2 * hl + x * hl, hl), hl)]
        return remote(ib, dst, sss.at[i], rss.at[i], dev(dest_y, dest_m))

    def state_send():
        return remote(hc_ref.at[_1 - x], hcv, sss.at[7], rss.at[7], dev(y, across))

    ib[...] = hc_ref[:, _0].astype(BF16)
    initv[:, _0, :, pl.ds(pl.multiple_of(c * _2 * hl + x * hl, hl), hl)] = ib[...]
    for i, (oy, om) in enumerate(everyone(y, m)):
        small(i, oy, om).start()
    state_send().start()
    for i in range(NX):
        xsend(i).start()

    loads[_0].wait()
    for t in range(xb.shape[_1] // LANES):
        cols = part(t, LANES)
        for b in range(BATCH):
            xf[t % 4, pl.ds(b, seq, stride=BATCH), :] = xin[b, :, cols].astype(F32)
        xb[:, cols] = xf[t % 4].astype(BF16)
    xout = local(xb, xt_hbm, osem.at[_0])
    xout.start()
    loads[4].wait()
    for t in range(per):
        cols = part(t, LANES)
        for b in range(BATCH):
            xf[t % 4, pl.ds(b, seq, stride=BATCH), :] = gyin[b, :, cols].astype(F32)
        gyb[:, cols] = xf[t % 4].astype(BF16)
    gout = local(gyb, gyt_hbm.at[_0], osem.at[_1])
    gout.start()

    def gy_send():
        return remote(gyb, gyt_hbm.at[_1], gsem.at[_0], gsem.at[_1], dev(y, across))

    @pl.when(x == _0)
    def _():
        gy_send().start()

    for cp in loads[_1:4]:
        cp.wait()

    def tiles(buf, raw, blk):
        spread[buf] = raw[aligned(blk, span), :].astype(F32)
        for g in GATES:
            for ct in range(per):
                yield g * hl + ct * LANES, spread[buf, pl.ds(ct * 4 + g, KB, stride=stride), :]

    def job_out(pos, blk, wo, wto):
        return (local(wst.at[pos], wo.at[aligned(blk, KB), :], jsem.at[pos, _0]),
                local(wtst.at[pos], wto.at[:, aligned(blk, KB)], jsem.at[pos, _1]))

    def job(pos, raw, blk, wo, wto):
        for off, tile in tiles(pos % _2, raw, blk):
            wst[pos, :, off:off + LANES] = tile.astype(BF16)
            wtst[pos, off:off + LANES, :] = tile.T.astype(BF16)
        for cp in job_out(pos, blk, wo, wto):
            cp.start()

    def job_wait(pos, wo, wto):
        for cp in job_out(pos, _0, wo, wto):
            cp.wait()

    early = NX // _2

    def body(i, _):
        @pl.when(i < early)
        def _():
            for q in range(4):
                blk = i * 4 + q
                for off, tile in tiles(q % _2, rin, blk):
                    win[aligned(blk, KB), off:off + LANES] = tile.astype(BF16)

        @pl.when(i == early)
        def _():
            row = gate_row(bias_ref, _0)
            nr = KB

            def pre_body(r, _):
                val = mm(xb[aligned(r, nr), :], win[...]) + row
                prev[aligned(r, nr // 8)] = val.reshape(nr // 8, 8, val.shape[_1])
                return _0

            lax.fori_loop(_0, xb.shape[_0] // nr, pre_body, _0)
            local(prev, pre_hbm, osem.at[_2]).start()

        @pl.when(i >= early)
        def _():
            for q in range(4):
                if q < _2:
                    @pl.when(i > early)
                    def _():
                        job_wait(q, wup2_hbm, wupt_hbm)
                else:
                    job_wait(q % _2, wup2_hbm, wupt_hbm)
                job(q % _2, rup, (i - early) * 4 + q, wup2_hbm, wupt_hbm)

        for q in range(_2):
            @pl.when(i > _0)
            def _():
                job_wait(_2 + q, wa_hbm, wat_hbm)
            job(_2 + q, ra, i * _2 + q, wa_hbm, wat_hbm)

        xsend(i).wait_recv()
        ysend(i).start()

        @pl.when(i > _0)
        def _():
            job_wait(4, wb_hbm, wbt_hbm)
        job(4, rb, y * NX + i, wb_hbm, wbt_hbm)

        @pl.when(i > _0)
        def _():
            ysend(i - _1).wait_recv()

            @pl.when(i > _1)
            def _():
                job_wait(5, wb_hbm, wbt_hbm)
            job(5, rb, (_1 - y) * NX + i - _1, wb_hbm, wbt_hbm)
        return _0

    lax.fori_loop(_0, NX, body, _0)
    job_wait(5, wb_hbm, wbt_hbm)
    ysend(NX - _1).wait_recv()
    job(5, rb, (_1 - y) * NX + NX - _1, wb_hbm, wbt_hbm)

    for i, (oy, om) in enumerate(everyone(y, m)):
        small(i, oy, om).wait()
    state_send().wait()
    hcb_ref[...] = hcv[...]
    init_ref[...] = initv[...]

    @pl.when(x == _0)
    def _():
        gy_send().wait_send()

    @pl.when(x == _1)
    def _():
        gy_send().wait_recv()

    for i in range(NX):
        xsend(i).wait_send()
        ysend(i).wait_send()
    for q in range(_2):
        job_wait(q, wup2_hbm, wupt_hbm)
        job_wait(_2 + q, wa_hbm, wat_hbm)
    job_wait(4, wb_hbm, wbt_hbm)
    job_wait(5, wb_hbm, wbt_hbm)
    xout.wait()
    gout.wait()
    local(prev, pre_hbm, osem.at[_2]).wait()


def fwd_kernel(wa_hbm, wb_hbm, wup_hbm, pre_hbm, xt_hbm, hc_ref, hcb_ref, bias_ref,
               act_hbm, cell_hbm, lown_hbm, loth_hbm, town_hbm, toth_hbm, xoth_hbm, last_ref, fin_ref,
               w, wup, prea, preb, actv, cellv, histv, hbuf, hch, cst, hs, hr,
               lsem, psem, osem, xs, xr, hss, hrs, ps, prs, csem, fsem):
    y, m, x, c = place()
    beside, across, skew = flips(m)
    nch = hbuf.shape[_0]
    npair = nch * PAIRS
    hl = hs.shape[3]
    half = _2 * hl
    wide = 4 * hl
    own_cols = pl.ds(pl.multiple_of(c * half, half), half)
    others = everyone(y, m)

    loads = []
    for pos, shard in enumerate((m, across, beside, skew)):
        for col, src in enumerate((wa_hbm, wb_hbm)):
            loads.append(local(src.at[aligned(shard, hl), :], w.at[pl.ds(pos * hl, hl), pl.ds(col * wide, wide)],
                               lsem.at[len(loads)]))
    up_loads = [local(wup_hbm.at[pl.ds(shard * hl, hl), :], wup.at[pl.ds(pos * hl, hl), :], lsem.at[8 + pos])
                for pos, shard in enumerate((_0, _2, _1, 3))]
    for cp in loads:
        cp.start()

    def pre_load(k):
        rows = pl.ds(k * PAIRS, PAIRS)
        return local(pre_hbm.at[rows], prea.at[rows], psem.at[k])

    @pl.when(x == _0)
    def _():
        def start(k, _):
            pre_load(k).start()
            return _0
        lax.fori_loop(_0, nch, start, _0)

    for cp in up_loads:
        cp.start()

    entry_barrier(y, m)

    def swap(slot, s):
        return remote(hs.at[slot, s], hr.at[slot, s], xs.at[slot, s], xr.at[slot, s], dev(y, beside))

    def pre_send(i):
        return remote(pre_hbm.at[i], preb.at[i], fsem.at[_0], prs.at[i], dev(y, across))

    def up_send(k, p):
        return remote(prea.at[npair + p], preb.at[k * PAIRS + p], ps.at[p], prs.at[k * PAIRS + p], dev(y, across))

    def x_send():
        return remote(xt_hbm, xoth_hbm, fsem.at[_1], fsem.at[_2], dev(_1 - y, m))

    @pl.when(x == _1)
    def _():
        def start(i, _):
            pre_send(i).start()
            return _0
        lax.fori_loop(_0, npair, start, _0)

    x_send().start()

    def low_send(k, i):
        oy, om = others[i]
        if i < 3:
            return remote(histv.at[k], hbuf.at[k, :, own_cols], hss.at[i], hrs.at[k, c], dev(oy, om))
        return remote(histv.at[k], loth_hbm.at[aligned(k, ROWS), own_cols], hss.at[i], csem.at[_0], dev(oy, om))

    def top_send(k, i):
        oy, om = others[i]
        dst, sem = (town_hbm, csem.at[_1]) if i < 3 else (toth_hbm, csem.at[_2])
        return remote(histv.at[k], dst.at[aligned(k, ROWS), own_cols], hss.at[i], sem, dev(oy, om))

    def hrecv(k, core):
        cols = pl.ds(pl.multiple_of(core * half, half), half)
        return remote(histv.at[k], hbuf.at[k, :, cols], hss.at[_0], hrs.at[k, core], dev(y, beside))

    def own_top(k):
        return local(histv.at[k], town_hbm.at[aligned(k, ROWS), own_cols], osem.at[3])

    init = [jnp.where(x == _0, hc_ref[_0], hc_ref[_1]), hcb_ref[...]]
    for s in BOTH:
        units = part(s, hl)
        hs[_0, s] = init[s][_0].astype(BF16)
        cst[:, units] = init[s][_1]
        cellv[_0, _0:4, units] = init[s][_1]
        cellv[_0, 4:8, units] = init[s][_1]
        swap(_0, s).start()
    for cp in loads:
        cp.wait()
    for cp in up_loads:
        cp.wait()

    def step(k, p, j, between):
        pair = k * PAIRS + p
        rows = part(j, BATCH)
        cols = (slice(_0, wide), slice(wide, _2 * wide))
        acc = [mm(hs[j, _0], w[_0:hl, cols[s]]) + mm(hs[j, _1], w[hl:half, cols[s]]) for s in BOTH]
        swap(j, _0).wait()
        swap(j, _1).wait()
        between()
        got = (hr[j, _0], hr[j, _1])
        acc = [acc[s] + (mm(got[_0], w[half:half + hl, cols[s]]) + mm(got[_1], w[half + hl:, cols[s]])) for s in BOTH]
        for s, pre in ((_0, prea), (_1, preb)):
            base = s * wide
            units = part(s, hl)

            def gate(g):
                return acc[s][:, part(g, hl)] + pre[pair, rows, part(g, hl)]

            gi = sigm(gate(_0))
            gf = sigm(gate(_1))
            go = sigm(gate(_2))
            gu = jnp.tanh(gate(3))
            cn = gf * cst[:, units] + gi * gu
            hn = go * jnp.tanh(cn)
            hs[_1 - j, s] = hn.astype(BF16)
            cst[:, units] = cn
            for g, val in enumerate((gi, gf, go, gu)):
                actv[pair, rows, part(g, hl, base)] = val
            cellv[pair + _1, rows, units] = cn
            hch[p, rows, units] = hn
        swap(_1 - j, _0).start()
        swap(_1 - j, _1).start()

    def up_product(k, at):
        prea[pl.ds(at, PAIRS)] = (mm(hbuf[k], wup[...]) + gate_row(bias_ref, _1)).reshape(PAIRS, 8, wide)

    def again(make, k, fresh):
        @pl.when(fresh)
        def _():
            make(k - _1).wait_send()
        make(k).start()

    def low_copy(i):
        return lambda k: low_send(k, i)

    def up_copy(p):
        return lambda k: up_send(k, p)

    low_turns = ((_1,), (_2,), ('up', _1), ('up', _2), ('up', 3), (3,), (4,), (5, 6))

    def turn(k, e):
        q = k - _1

        @pl.when((x == _0) & (q >= _0))
        def _():
            if low_turns[e][_0] == 'up':
                up_copy(low_turns[e][_1])(q).start()
            else:
                for i in low_turns[e]:
                    again(low_copy(i), q, q >= _1)

        if e < 7:
            @pl.when((x == _1) & (q >= _0))
            def _():
                again(lambda kk: top_send(kk, e), q, q >= _1)

    def act_out(k):
        rows = pl.ds(k * PAIRS, PAIRS)
        return local(actv.at[rows], act_hbm.at[rows], osem.at[_0])

    def slot_body(s, _):
        k = s - x
        live = (k >= _0) & (k < nch)
        final = (x == _0) & (s == nch)
        upper = (x == _1) & live

        @pl.when(upper)
        def _():
            hrecv(k, c).wait_recv()

        @pl.when(upper | final)
        def _():
            q = x * k + (_1 - x) * (nch - _1)
            hrecv(q, _1 - c).wait_recv()

            @pl.when(final)
            def _():
                for i in (_1, _2):
                    again(low_copy(i), nch - _1, True)
                for p in range(PAIRS):
                    up_send(nch - _2, p).wait_send()
            up_product(q, x * k * PAIRS + (_1 - x) * npair)

            @pl.when(final)
            def _():
                for p in range(PAIRS):
                    up_send(nch - _1, p).start()
                for i in range(3, 7):
                    again(low_copy(i), nch - _1, True)

        @pl.when(live)
        def _():
            @pl.when(x == _0)
            def _():
                pre_load(k).wait()

            up_send(k, _0).wait_recv()
            step(k, _0, _0, lambda: turn(k, _0))

            @pl.when((x == _0) & (k >= _1))
            def _():
                hrecv(k - _1, _1 - c).wait_recv()

                @pl.when(k >= _2)
                def _():
                    for p in range(PAIRS):
                        up_send(k - _2, p).wait_send()
                up_product(k - _1, npair)
                up_send(k - _1, _0).start()

            step(k, _0, _1, lambda: turn(k, _1))

            def pair_body(p, _):
                def turn_of(j):
                    for pp in range(_1, PAIRS):
                        @pl.when(p == pp)
                        def _():
                            turn(k, _2 * pp + j)

                up_send(k, p).wait_recv()
                step(k, p, _0, lambda: turn_of(_0))
                step(k, p, _1, lambda: turn_of(_1))
                return _0

            lax.fori_loop(_1, PAIRS, pair_body, _0)
            act_out(k).start()

            @pl.when(x == _0)
            def _():
                block = hch[...].reshape(ROWS, half).astype(BF16)
                histv[k] = block
                hbuf[k, :, own_cols] = block

                again(low_copy(_0), k, k >= _1)

            @pl.when(x == _1)
            def _():
                block = hch[...].reshape(ROWS, half).astype(BF16)
                histv[k, :, _0:hl] = block[:, hl:half]
                histv[k, :, hl:half] = block[:, _0:hl]

                own_top(k).start()
        return _0

    lax.fori_loop(_0, nch + _1, slot_body, _0)
    local(cellv, cell_hbm, osem.at[_2]).start()
    swap(_0, _0).wait()
    swap(_0, _1).wait()
    last_ref[...] = histv[nch - _1]
    for s in BOTH:
        fin_ref[s, _0] = hch[PAIRS - _1, 4:8, part(s, hl)]
        fin_ref[s, _1] = cst[:, part(s, hl)]

    sent = pl.ds(_0, (nch - _1) * ROWS)

    @pl.when(x == _0)
    def _():
        for i in range(7):
            low_send(nch - _1, i).wait_send()
        for p in range(PAIRS):
            up_send(nch - _1, p).wait_send()
        whole = town_hbm.at[sent, :]
        local(whole, whole, csem.at[_1]).wait()

    @pl.when(x == _1)
    def _():
        for i in range(7):
            top_send(nch - _2, i).wait_send()
        local(pre_hbm, pre_hbm, fsem.at[_0]).wait()
        part = town_hbm.at[sent, pl.ds(_0, half)]
        local(part, part, csem.at[_1]).wait()
        mine = town_hbm.at[:, pl.ds(_0, half)]
        local(mine, mine, osem.at[3]).wait()

    def low_out(k):
        return local(hbuf.at[k], lown_hbm.at[aligned(k, ROWS), :], osem.at[_1])

    def low_start(k, _):
        low_out(k).start()
        return _0

    lax.fori_loop(_0, nch, low_start, _0)
    local(loth_hbm, loth_hbm, csem.at[_0]).wait()
    far = toth_hbm.at[sent, :]
    local(far, far, csem.at[_2]).wait()
    x_send().wait()
    local(lown_hbm, lown_hbm, osem.at[_1]).wait()
    local(cellv, cell_hbm, osem.at[_2]).wait()
    local(actv, act_hbm, osem.at[_0]).wait()


def bwd_kernel(wta_hbm, wtb_hbm, wupt_hbm, act_hbm, cell_hbm, gy_hbm, last_ref, fin_ref,
               dg_hbm, tlo_hbm, tlf_hbm, bias_ref, hfin_ref, cfin_ref,
               wt, wupt, actv, cellv, dout, gyv, dgv, dgr, dgch, dgs, dct, bacc, own, snd, rcv, pin, pout, bsnd, brcv, finr,
               lsem, asem, osem, xs, xr, gs, grs, ps, prs, csem, bsem, tsem):
    y, m, x, c = place()
    beside, across, skew = flips(m)
    nch = dgv.shape[_0]
    half = dct.shape[_1]
    hl = half // _2
    wide = 4 * hl
    hp = PAIRS // _2
    hr = ROWS // _2

    first_loads = [local(cell_hbm, cellv, lsem.at[12])]
    loads = []
    for pos, shard in enumerate((beside, skew, m, across)):
        for row, src in enumerate((wta_hbm, wtb_hbm)):
            loads.append(local(src.at[:, aligned(shard, hl)], wt.at[pl.ds(row * wide, wide), pl.ds(pos * hl, hl)],
                               lsem.at[len(loads)]))
    up_loads = [local(wupt_hbm.at[:, aligned(shard, hl)], wupt.at[:, pl.ds(pos * hl, hl)], lsem.at[8 + pos])
                for pos, shard in enumerate((_1 - c, 3 - c, c, _2 + c))]

    def act_in(k):
        rows = pl.ds(k * PAIRS, PAIRS)
        return local(act_hbm.at[rows], actv.at[rows], asem.at[k])

    @pl.when(x == _1)
    def _():
        local(gy_hbm, gyv, lsem.at[13]).start()
    for cp in first_loads:
        cp.start()
    act_in(nch - _1).start()
    for cp in loads + up_loads:
        cp.start()

    def start_act(i, _):
        act_in(nch - _2 - i).start()
        return _0

    lax.fori_loop(_0, nch - _1, start_act, _0)
    entry_barrier(y, m)

    own_cols = pl.ds(pl.multiple_of(c * half, half), half)

    def last_sends():
        return [remote(last_ref, (tlo_hbm if i < 3 else tlf_hbm).at[:, own_cols], tsem.at[i],
                       tsem.at[9] if i < 3 else tsem.at[10], dev(oy, om))
                for i, (oy, om) in enumerate(everyone(y, m))]

    def last_keep():
        return local(last_ref, tlo_hbm.at[:, own_cols], tsem.at[11])

    def fin_send():
        return remote(fin_ref.at[_1], finr, tsem.at[7], tsem.at[8], dev(y, across))

    @pl.when(x == _1)
    def _():
        for cp in last_sends():
            cp.start()
        last_keep().start()
    fin_send().start()

    def swap(slot):
        return remote(snd.at[slot], rcv.at[slot], xs.at[slot], xr.at[slot], dev(y, beside))

    part_a = pl.ds(_0, wide)
    part_b = pl.ds(wide, wide)

    def half_rows(k, h):
        return pl.ds(pl.multiple_of(k * ROWS, ROWS) + h * hr, hr)

    def up_grads(k, h):
        rows = pl.ds(h * hr, hr)
        return remote(dgv.at[k, rows, part_b], dgr.at[k, rows], gs.at[_0, h], grs.at[k, h], dev(y, across))

    def near(k, h, top):
        if top:
            return up_grads(k, h)
        return remote(dgv.at[k, pl.ds(h * hr, hr), part_b], dg_hbm.at[_0, _0, half_rows(k, h), :],
                      gs.at[_0, h], csem.at[_2], dev(y, across))

    def wider(k, h, top):
        rows = pl.ds(h * hr, hr)
        layer = _1 if top else _0
        dst = dg_hbm.at[layer, _1, half_rows(k, h), :]
        return (remote(dgv.at[k, rows, part_a], dst, gs.at[_1, h], csem.at[_0], dev(_1 - y, m)),
                remote(dgv.at[k, rows, part_b], dst, gs.at[_2, h], csem.at[_1], dev(_1 - y, across)))

    def keep(k, h, top):
        return local(dgv.at[k, pl.ds(h * hr, hr), part_a], dg_hbm.at[_1 if top else _0, _0, half_rows(k, h), :], osem.at[_0])

    def keep_up(k):
        return local(dgr.at[k], dg_hbm.at[_1, _0, aligned(k, ROWS), :], osem.at[_1])

    def psend(k, pos, piece, dest, src):
        rows = pl.ds(piece * hp, hp)
        return remote(pout.at[pos, rows], pin.at[src, k, rows], ps.at[pos, piece], prs.at[src, k, piece], dev(y, dest))

    def up_sends(k, pos):
        return [psend(k, pos, piece, skew if pos == _0 else across, c) for piece in (_1, _0)]

    def side_sends(k):
        return [psend(k, _0, piece, beside, _2) for piece in (_1, _0)]

    dct[...] = jnp.zeros(dct.shape, F32)
    bacc[...] = jnp.zeros(bacc.shape, F32)

    @pl.when(x == _1)
    def _():
        local(gy_hbm, gyv, lsem.at[13]).wait()
        for s in BOTH:
            dout[:, :, part(s, hl)] = gyv[s].astype(F32).reshape(nch * PAIRS, 8, hl)

    @pl.when(x == _0)
    def _():
        for cp in up_loads:
            cp.wait()
    for cp in first_loads:
        cp.wait()

    def point(k, p, j, inner):
        pair = k * PAIRS + p
        rows = part(j, BATCH)
        for s in BOTH:
            base = s * wide
            units = part(s, hl)
            gi, gf, go, gu = (actv[pair, rows, part(g, hl, base)] for g in GATES)
            tc = jnp.tanh(cellv[pair + _1, rows, units])
            cp = cellv[pair + _1, _0:4, units] if j else cellv[pair, 4:8, units]
            dh = dout[pair, rows, units]
            if inner:
                dh = dh + own[:, units] + rcv[j, :, units]
            dc = dct[:, units] + dh * go * (1.0 - tc * tc)
            dct[:, units] = dc * gf
            grads = (dc * gu * gi * (1.0 - gi), dc * cp * gf * (1.0 - gf),
                     dh * tc * go * (1.0 - go), dc * gi * (1.0 - gu * gu))
            for g, val in enumerate(grads):
                cols = part(g, hl, base)
                dgs[:, cols] = val.astype(BF16)
                dgch[p, rows, cols] = val

    def step(k, p, j, after):
        dgl = dgs[...]
        snd[j] = mm(dgl, wt[:, _0:half])
        swap(j).start()
        own[...] = mm(dgl, wt[:, half:])
        swap(j).wait()
        after()
        point(k, p, j, True)

    def again(make, k):
        @pl.when(k < nch - _1)
        def _():
            make(k + _1).wait_send()
        make(k).start()

    def near_copy(h, top):
        return lambda k: near(k, h, top)

    def wide_copy(h, top, i):
        return lambda k: wider(k, h, top)[i]

    def turn(k, e):
        late = k < nch - _1

        if e < 3:
            @pl.when((x == _0) & late)
            def _():
                again((near_copy(_0, False), wide_copy(_0, False, _0), wide_copy(_0, False, _1))[e], k + _1)
        if e in (4, 5, 6):
            @pl.when(x == _0)
            def _():
                again((near_copy(_1, False), wide_copy(_1, False, _0), wide_copy(_1, False, _1))[e - 4], k)
        if e < _2:
            @pl.when((x == _1) & late)
            def _():
                up_sends(k + _1, e)[_1].start()
        if e in (_2, 3):
            @pl.when((x == _1) & late)
            def _():
                again(wide_copy(_0, True, e - _2), k + _1)
        if e in (5, 6):
            @pl.when(x == _1)
            def _():
                again(wide_copy(_1, True, e - 5), k)

    def emit(k, h):
        dgv[k, part(h, hr), :] = dgch[part(h, hp)].reshape(hr, _2 * wide).astype(BF16)
        total = dgch[h * hp]
        for p in range(h * hp + _1, (h + _1) * hp):
            total = total + dgch[p]
        bacc[...] += total

        @pl.when(x == _0)
        def _():
            keep(k, h, False).start()

        @pl.when(x == _1)
        def _():
            again(near_copy(h, True), k)
            keep(k, h, True).start()

    def take(k, piece):
        for src in (_0, _1, _2):
            psend(k, _0, piece, beside, src).wait_recv()
        rows = pl.ds(piece * hp, hp)
        dout[pl.ds(k * PAIRS + piece * hp, hp)] = pout[_1, rows] + pin[_0, k, rows] + pin[_1, k, rows] + pin[_2, k, rows]

    def slot_body(s, _):
        k = nch - _1 - s + (_1 - x)
        live = (k >= _0) & (k < nch)
        first = live & (k == nch - _1)

        @pl.when((x == _0) & live)
        def _():
            @pl.when(k < nch - _1)
            def _():
                for cp in side_sends(k + _1):
                    cp.wait_send()
            up_grads(k, _1).wait_recv()
            up_grads(k, _0).wait_recv()
            keep_up(k).start()
            block = dgr[k]
            pout[_0] = mm(block, wupt[:, _0:half]).reshape(PAIRS, 8, half)
            for cp in side_sends(k):
                cp.start()
            pout[_1] = mm(block, wupt[:, half:]).reshape(PAIRS, 8, half)
            take(k, _1)

        @pl.when(live)
        def _():
            act_in(k).wait()

            @pl.when(first)
            def _():
                point(k, PAIRS - _1, _1, False)
                for cp in loads:
                    cp.wait()

                @pl.when(x == _1)
                def _():
                    for cp in up_loads:
                        cp.wait()

            @pl.when(k < nch - _1)
            def _():
                step(k, PAIRS - _1, _1, lambda: turn(k, _0))
            step(k, PAIRS - _1, _0, lambda: turn(k, _1))

            def pair_body(i, _):
                p = PAIRS - _2 - i

                @pl.when((x == _0) & (p == hp - _1))
                def _():
                    take(k, _0)

                def turn_of(j):
                    for pp in range(PAIRS - _1):
                        @pl.when(p == pp)
                        def _():
                            turn(k, _2 * (PAIRS - _1 - pp) + _1 - j)

                step(k, p, _1, lambda: turn_of(_1))
                step(k, p, _0, lambda: turn_of(_0))

                @pl.when(p == hp)
                def _():
                    emit(k, _1)
                return _0

            lax.fori_loop(_0, PAIRS - _1, pair_body, _0)
            emit(k, _0)

        @pl.when((x == _1) & live)
        def _():
            @pl.when(k < nch - _1)
            def _():
                for pos in BOTH:
                    for cp in up_sends(k + _1, pos):
                        cp.wait_send()
            block = dgv[k, :, _0:wide]
            for pos in BOTH:
                pout[pos] = mm(block, wupt[:, part(pos, half)]).reshape(PAIRS, 8, half)
                up_sends(k, pos)[_0].start()
        return _0

    lax.fori_loop(_0, nch + _1, slot_body, _0)

    @pl.when(x == _0)
    def _():
        again(near_copy(_0, False), _0)
        for i in BOTH:
            again(wide_copy(_0, False, i), _0)

    @pl.when(x == _1)
    def _():
        for pos in BOTH:
            up_sends(_0, pos)[_1].start()
        for i in BOTH:
            again(wide_copy(_0, True, i), _0)

    bsnd[_0] = bacc[:, _0:wide]
    bsnd[_1] = bacc[:, wide:]
    shares = (remote(bsnd.at[_0], brcv.at[_0], bsem.at[_0], bsem.at[3], dev(_1 - y, m)),
              remote(bsnd.at[_1], brcv.at[_1], bsem.at[_1], bsem.at[4], dev(y, across)),
              remote(bsnd.at[_1], brcv.at[_2], bsem.at[_2], bsem.at[5], dev(_1 - y, across)))
    for cp in shares:
        cp.start()

    fin_send().wait()
    for ref, i in ((hfin_ref, _0), (cfin_ref, _1)):
        ref[_0] = jnp.where(x == _0, fin_ref[_0, i], finr[i])
        ref[_1] = jnp.where(x == _0, finr[i], fin_ref[_0, i])

    quarter = dg_hbm.at[_0, _0]

    @pl.when(x == _0)
    def _():
        for cp in side_sends(_0):
            cp.wait_send()
        for h in BOTH:
            near(_0, h, False).wait_send()
            for cp in wider(_0, h, False):
                cp.wait_send()
        local(quarter, quarter, osem.at[_1]).wait()
        local(tlo_hbm, tlo_hbm, tsem.at[9]).wait()

    @pl.when(x == _1)
    def _():
        for pos in BOTH:
            for cp in up_sends(_0, pos):
                cp.wait_send()
        for h in BOTH:
            near(_0, h, True).wait_send()
            for cp in wider(_0, h, True):
                cp.wait_send()
        local(quarter, quarter, csem.at[_2]).wait()
        for cp in last_sends():
            cp.wait_send()
        local(last_ref, last_ref, tsem.at[9]).wait()
        last_keep().wait()

    local(tlf_hbm, tlf_hbm, tsem.at[10]).wait()
    local(quarter, quarter, csem.at[_0]).wait()
    local(quarter, quarter, csem.at[_1]).wait()
    local(quarter, quarter, osem.at[_0]).wait()
    for cp in shares:
        cp.wait()
    same = jnp.sum(bsnd[_0] + brcv[_0], axis=_0, keepdims=True)
    cross = jnp.sum(brcv[_1] + brcv[_2], axis=_0, keepdims=True)
    low = jnp.where(x == _0, same, cross)
    top = jnp.where(x == _0, cross, same)
    for g in GATES:
        bias_ref[_0, g:g + _1, :] = low[:, part(g, hl)]
        bias_ref[_1, g:g + _1, :] = top[:, part(g, hl)]


def grad_kernel(xo_hbm, xf_hbm, lo_hbm, lf_hbm, to_hbm, tf_hbm, tlo_hbm, tlf_hbm, init_ref, dg_hbm,
                dwin_hbm, dwup_hbm, dwrec_hbm, y_ref,
                lhs, grads, htop, shf, yf, lhst0, lhst1, pieces0, pieces1, lsem, osem):
    hidden = htop.shape[_1]
    srows = lo_hbm.shape[_0]
    lhst = (lhst0, lhst1)
    pieces = (pieces0, pieces1)
    kb = lhst0.shape[_0]
    hl = hidden // 4
    nblk = hidden // kb
    per = hl // LANES
    nq = hl // kb
    m = lax.axis_index('model')
    x = m // _2
    c = m % _2
    lo = pl.ds(_0, srows)
    hi = pl.ds(srows, srows)
    body_rows = pl.ds(_0, srows - ROWS)
    srcs = ((xo_hbm, lhs.at[_0, lo, :]), (xf_hbm, lhs.at[_0, hi, :]), (dg_hbm.at[_0, _0], grads.at[_0, lo, :]), (dg_hbm.at[_0, _1], grads.at[_0, hi, :]),
            (lo_hbm, lhs.at[_1, lo, :]), (lf_hbm, lhs.at[_1, hi, :]), (dg_hbm.at[_1, _0], grads.at[_1, lo, :]), (dg_hbm.at[_1, _1], grads.at[_1, hi, :]),
            (to_hbm.at[body_rows, :], htop.at[body_rows, :]),
            (tf_hbm.at[body_rows, :], htop.at[pl.ds(srows, srows - ROWS), :]),
            (tlo_hbm, htop.at[pl.ds(srows - ROWS, ROWS), :]), (tlf_hbm, htop.at[pl.ds(_2 * srows - ROWS, ROWS), :]))
    loads = [local(a, b, lsem.at[i]) for i, (a, b) in enumerate(srcs)]
    for cp in loads:
        cp.start()

    def core_row(i):
        q = i // nq
        return ((q % _2) * _2 + q // _2) * nq + i % nq

    def out_start(slot, n):
        ph = n // nblk
        i = lax.rem(n, nblk)

        def put(dst, off):
            for j in range(4 * per):
                local(pieces[slot].at[j], dst.at[aligned(off, kb), j, :], osem.at[slot]).start()

        @pl.when(ph == _0)
        def _():
            put(dwin_hbm, i)

        @pl.when(ph == _1)
        def _():
            put(dwup_hbm, core_row(i))

        @pl.when(ph >= _2)
        def _():
            put(dwrec_hbm, (ph - _2) * nblk + core_row(i))

    def out_wait(slot):
        local(pieces[slot], pieces[slot], osem.at[slot]).wait()

    def shift(src, dst, layer, i):
        cols = aligned(i, kb)
        for part in BOTH:
            base = part * srows
            shf[base + 4:base + srows, :] = src[pl.ds(base, srows), cols].astype(F32)[:srows - 4]
            shf[base:base + 4, :] = init_ref[layer, part, :, cols].astype(F32)
        dst[:, cols] = shf[...].astype(BF16)

    def prepare(slot, n):
        lhst[slot][...] = lhs[n // nblk, :, aligned(lax.rem(n, nblk), kb)].T

    total = 4 * nblk
    for cp in loads[_0:4]:
        cp.wait()
    prepare(_0, _0)

    def body(it, _):
        @pl.when(it == nblk // _2 - _1)
        def _():
            for cp in loads[4:]:
                cp.wait()

        @pl.when((it >= nblk // _2) & (it < nblk))
        def _():
            for e in BOTH:
                i = _2 * it + e - nblk
                shift(lhs.at[_1], lhs.at[_2], _0, i)
                shift(htop, lhs.at[3], _1, i)

        for e in BOTH:
            n = _2 * it + e

            @pl.when(n >= _2)
            def _():
                out_wait(e)
            res = mm(lhst[e][...], grads[lax.rem(n // nblk, _2)])
            for g in GATES:
                for ct in range(per):
                    col = g * hl + ct * LANES
                    pieces[e][ct * 4 + g] = res[:, col:col + LANES]
            prepare(_1 - e, jnp.minimum(n + _1, total - _1))
            out_start(e, n)
        return _0

    lax.fori_loop(_0, total // _2, body, _0)
    for t in range(per):
        yf[t] = htop[_0:srows, pl.ds(pl.multiple_of(c * _2 * hl + x * hl + t * LANES, LANES), LANES)].astype(F32)
        for b in range(BATCH):
            y_ref[b, :, part(t, LANES)] = yf[t, pl.ds(b, srows // BATCH, stride=BATCH), :].astype(BF16)
    for slot in BOTH:
        out_wait(slot)


def any_spec():
    return pl.BlockSpec(memory_space=pl.ANY)


def vmem_spec():
    return pl.BlockSpec(memory_space=pltpu.VMEM)


def sds(shape, dtype):
    return jax.ShapeDtypeStruct(shape, dtype)


DMA = pltpu.SemaphoreType.DMA


def comm_params(i):
    return pltpu.CompilerParams(collective_id=i, has_side_effects=True, vmem_limit_bytes=VMEM_LIMIT)


def run_prep(wrec, wup, win, x, gy, hc, bias):
    batch, seq, width = x.shape
    hl = gy.shape[_2]
    wide = 4 * hl
    hidden = 4 * hl
    rows = batch * seq
    raw = win.shape[_0]
    per = hl // LANES
    span = KB * 4 * per
    square = sds((hidden, wide), BF16)
    vm = pltpu.VMEM
    return pl.pallas_call(
        prep_kernel,
        name='lstm_prepare',
        out_shape=(square,) * 6 + (sds((rows // 8, 8, wide), F32), sds((rows, width), BF16), sds((_2, rows, hl), BF16),
                                   sds((_2, 4, hl), F32), sds((_2, _2, 4, hidden), BF16)),
        in_specs=[any_spec()] * 5 + [vmem_spec()] * _2,
        out_specs=(any_spec(),) * 9 + (vmem_spec(),) * _2,
        scratch_shapes=[
            vm((raw, LANES), BF16), vm((raw, LANES), BF16), vm((raw, LANES), BF16), vm((raw, LANES), BF16),
            vm((_2, span, LANES), F32), vm((6, KB, wide), BF16), vm((6, wide, KB), BF16), vm((width, wide), BF16),
            vm(x.shape, BF16), vm((4, rows, LANES), F32), vm((rows, width), BF16), vm((rows // 8, 8, wide), F32),
            vm(gy.shape, BF16), vm((rows, hl), BF16), vm((_2, 4, hl), BF16),
            vm((_2, _2, 4, hidden), BF16), vm((_2, 4, hl), F32),
            DMA((5,)), DMA((3,)), DMA((6, _2)), DMA((NX,)), DMA((NX,)), DMA((NX,)), DMA((NX,)), DMA((8,)), DMA((8,)), DMA((_2,)),
        ],
        compiler_params=comm_params(_0),
    )(wrec, wup, win, x, gy, hc, bias)


def run_fwd(wa, wb, wup, pre, xt, hc, hcb, bias):
    hidden, wide = wa.shape
    hl = wide // 4
    half = _2 * hl
    npair = pre.shape[_0]
    nch = npair // PAIRS
    rows = npair * 8
    hist = sds((rows, hidden), BF16)
    vm = pltpu.VMEM
    return pl.pallas_call(
        fwd_kernel,
        name='lstm_forward',
        out_shape=(sds((npair, 8, _2 * wide), F32), sds((npair + _1, 8, half), F32), hist, hist, hist, hist,
                   sds(xt.shape, BF16), sds((ROWS, half), BF16), sds((_2, _2, 4, hl), F32)),
        in_specs=[any_spec()] * 5 + [vmem_spec()] * 3,
        out_specs=(any_spec(),) * 7 + (vmem_spec(),) * _2,
        scratch_shapes=[
            vm((hidden, _2 * wide), BF16), vm((hidden, wide), BF16),
            vm((npair + PAIRS, 8, wide), F32), vm((npair, 8, wide), F32),
            vm((npair, 8, _2 * wide), F32), vm((npair + _1, 8, half), F32),
            vm((nch, ROWS, half), BF16), vm((nch, ROWS, hidden), BF16),
            vm((PAIRS, 8, half), F32), vm((4, half), F32),
            vm((_2, _2, 4, hl), BF16), vm((_2, _2, 4, hl), BF16),
            DMA((12,)), DMA((nch,)), DMA((4,)), DMA((_2, _2)), DMA((_2, _2)), DMA((7,)), DMA((nch, _2)),
            DMA((PAIRS,)), DMA((npair,)), DMA((3,)), DMA((3,)),
        ],
        compiler_params=comm_params(_1),
    )(wa, wb, wup, pre, xt, hc, hcb, bias)


def run_bwd(wta, wtb, wupt, act, cell, gy, last, fin):
    wide, hidden = wta.shape
    hl = wide // 4
    half = _2 * hl
    npair = act.shape[_0]
    nch = npair // PAIRS
    rows = npair * 8
    vm = pltpu.VMEM
    state = sds((_2, 4, hl), F32)
    return pl.pallas_call(
        bwd_kernel,
        name='lstm_backward',
        out_shape=(sds((_2, _2, rows, wide), BF16), sds((ROWS, hidden), BF16), sds((ROWS, hidden), BF16), state, state, state),
        in_specs=[any_spec()] * 6 + [vmem_spec()] * _2,
        out_specs=(any_spec(),) * 3 + (vmem_spec(),) * 3,
        scratch_shapes=[
            vm((_2 * wide, hidden), BF16), vm((wide, hidden), BF16),
            vm((npair, 8, _2 * wide), F32), vm((npair + _1, 8, half), F32),
            vm((npair, 8, half), F32), vm((_2, rows, hl), BF16),
            vm((nch, ROWS, _2 * wide), BF16), vm((nch, ROWS, wide), BF16),
            vm((PAIRS, 8, _2 * wide), F32), vm((4, _2 * wide), BF16),
            vm((4, half), F32), vm((8, _2 * wide), F32),
            vm((4, half), F32), vm((_2, 4, half), F32), vm((_2, 4, half), F32),
            vm((3, nch, PAIRS, 8, half), F32), vm((_2, PAIRS, 8, half), F32),
            vm((_2, 8, wide), F32), vm((3, 8, wide), F32), vm((_2, 4, hl), F32),
            DMA((14,)), DMA((nch,)), DMA((_2,)), DMA((_2,)), DMA((_2,)), DMA((3, _2)), DMA((nch, _2)), DMA((_2, _2)), DMA((3, nch, _2)),
            DMA((3,)), DMA((6,)), DMA((12,)),
        ],
        compiler_params=comm_params(_2),
    )(wta, wtb, wupt, act, cell, gy, last, fin)


def run_grads(xo, xf, lo, lf, to, tf, tlo, tlf, init, dg):
    srows, hidden = lo.shape
    rows = _2 * srows
    wide = dg.shape[3]
    tile = (wide // LANES, LANES)
    hl = wide // 4
    kb = 512
    vm = pltpu.VMEM
    return pl.pallas_call(
        grad_kernel,
        name='weight_grads',
        out_shape=(sds((hidden,) + tile, F32), sds((hidden,) + tile, F32), sds((_2 * hidden,) + tile, F32),
                   sds((BATCH, srows // BATCH, hl), BF16)),
        in_specs=[any_spec()] * 8 + [vmem_spec(), any_spec()],
        out_specs=(any_spec(),) * 3 + (vmem_spec(),),
        scratch_shapes=[vm((4, rows, hidden), BF16), vm((_2, rows, wide), BF16), vm((rows, hidden), BF16),
                        vm((rows, kb), F32), vm((hl // LANES, srows, LANES), F32), vm((kb, rows), BF16), vm((kb, rows), BF16),
                        vm((wide // LANES, kb, LANES), F32), vm((wide // LANES, kb, LANES), F32), DMA((12,)), DMA((_2,))],
        compiler_params=pltpu.CompilerParams(vmem_limit_bytes=VMEM_LIMIT),
    )(xo, xf, lo, lf, to, tf, tlo, tlf, init, dg)


def to_raw(w):
    hl = w.shape[-_1]
    w = w.reshape(-_1, 4, hl // LANES, LANES)
    return jnp.swapaxes(w, _1, _2).reshape(-_1, LANES)


def from_raw(v, lead, hl):
    v = v.reshape(-_1, hl // LANES, 4, LANES)
    return jnp.swapaxes(v, _1, _2).reshape(lead + (-_1, 4, hl))


def solution(mesh):
    batch_axes = ('part', 'data')
    seq_spec = P(batch_axes, None, 'model')
    state_spec = P(None, batch_axes, 'model')
    weight_spec = P(None, None, None, 'model')
    in_specs = (P(batch_axes, None, None), seq_spec, state_spec, state_spec,
                P(None, None, 'model'), weight_spec, weight_spec, P(None, None, 'model'))
    out_specs = (seq_spec, state_spec, state_spec, P('part', None, 'model'),
                 P(None, 'part', None, 'model'), P(None, 'part', None, 'model'), P(None, 'part', 'model'))

    def local_program(x_seq, gy_seq, h_init, c_init, w_in, w_up, w_rec, gate_bias):
        hl = w_in.shape[_2]
        hc = jnp.stack([h_init, c_init], axis=_1)
        wa, wb, wat, wbt, wup, wupt, pre, xt, gyt, hcb, init = run_prep(
            to_raw(w_rec), to_raw(w_up), to_raw(w_in), x_seq, gy_seq, hc, gate_bias)
        act, cell, low_own, low_far, top_own, top_far, x_far, last, fin = run_fwd(
            wa, wb, wup, pre, xt, hc, hcb, gate_bias)
        dg, last_own, last_far, bias, h_last, c_last = run_bwd(wat, wbt, wupt, act, cell, gyt, last, fin)
        dw_in, dw_up, dw_rec, y_out = run_grads(
            xt, x_far, low_own, low_far, top_own, top_far, last_own, last_far, init, dg)
        return (y_out, h_last, c_last, from_raw(dw_in, (), hl), from_raw(dw_up, (_1,), hl),
                from_raw(dw_rec, (_2,), hl), bias)

    return jax.shard_map(local_program, mesh=mesh, in_specs=in_specs, out_specs=out_specs, check_vma=False)
```

time: 978 us -> 940 us (0.961)
  Pallas kernels: 974 us -> 935 us
    pallas_call x2, Pallas kernels: 455 us -> 435 us  [the longest x1 386 us: run_bwd(): pl.pallas_call(bwd_kernel, name='lstm_backward', out_shape=(sds((_2, _2,...]
    pallas_call x1, Pallas kernels: 406 us -> 388 us  [run_fwd(): pl.pallas_call(fwd_kernel, name='lstm_forward', out_shape=(sds((npair, 8,...]
where the time goes in v3:
time: 940 us; the launch traced here: 939 us
  Pallas kernels  935 us (99%)
    pallas_call x1, Pallas kernels, run_fwd(): pl.pallas_call(fwd_kernel, name='lstm_forward', out_shape=(sds((npair, 8,...  388 us
    pallas_call x1, Pallas kernels, run_bwd(): pl.pallas_call(bwd_kernel, name='lstm_backward', out_shape=(sds((_2, _2,...  386 us
    pallas_call x1, Pallas kernels, run_prep(): pl.pallas_call(prep_kernel, name='lstm_prepare', out_shape=(square,) * 6...  112 us
    pallas_call x1, Pallas kernels, run_grads(): pl.pallas_call(grad_kernel, name='weight_grads', out_shape=(sds((hidden,)...  49.2 us

profile of v3, /device:TPU:0, one launch (start us, length us, event | category | flops | bytes accessed | tf_op | source)
XLA Modules:
  0.0 939.2 jit_solution(481714648388376300)
XLA Ops:
  0.6 1.4 pad_maximum_fusion.hc_ref
  2.0 112.3 %lstm_prepare.1 = (bf16[2048,2048]{1,0:T(8,128)(2,1)}, bf16[2048,2048]{1,0:T(8,128)(2,1)}, bf16[2048,2048]{1,0:T(8,128)(2,1)}, bf16[2048,2048]{1,0:T(8,128)(2,1)...) custom-call(bf16[65536,128]{1,0:T(8,128)(2,1)} %bitcast.32, ...), custom_call_target="tpu_custom_call" | custom-call | tf_op jit(solution)/shard_map/lstm_prepare/pallas_call | solution.py:1052
  114.3 388.2 %lstm_forward.1 = (f32[64,8,4096]{2,1,0:T(8,128)}, f32[65,8,1024]{2,1,0:T(8,128)}, bf16[512,2048]{1,0:T(8,128)(2,1)}, bf16[512,2048]{1,0:T(8,128)(2,1)}, bf16[51...) custom-call(bf16[2048,2048]{1,0:T(8,128)(2,1)} %get-tuple-element.38, ...), custom_call_target="tpu_custom_call" | custom-call | tf_op jit(solution)/shard_map/lstm_forward/pallas_call | solution.py:1080
  502.5 385.6 %lstm_backward.1 = (bf16[2,2,512,2048]{3,2,1,0:T(8,128)(2,1)}, bf16[32,2048]{1,0:T(8,128)(2,1)}, bf16[32,2048]{1,0:T(8,128)(2,1)}, f32[2,4,512]{2,1,0:T(4,128)},...) custom-call(bf16[2048,2048]{1,0:T(8,128)(2,1)} %get-tuple-element.48.wta_hbm, bf16[2048,2048]{1,0:T(8,128)(2,1)} %get-tuple-element.49.wtb_hbm, ...), custom_call_target="tpu_custom_call" | custom-call | tf_op jit(solution)/shard_map/lstm_backward/pallas_call | solution.py:1110
  888.2 0.0 copy-start.2
  888.2 0.0 copy-start.1
  888.2 0.0 copy-start
  888.2 49.2 %weight_grads.1 = (f32[2048,16,128]{2,1,0:T(8,128)}, f32[2048,16,128]{2,1,0:T(8,128)}, f32[4096,16,128]{2,1,0:T(8,128)}, bf16[4,128,512]{2,1,0:T(8,128)(2,1)}) custom-call(bf16[512,2048]{1,0:T(8,128)(2,1)} %get-tuple-element.37.xt_hbm.xo_hbm, bf16[512,2048]{1,0:T(8,128)(2,1)} %get-tuple-element.43.xf_hbm, bf16[512,2048]{1,0:T(8,128)(2,1)} %get-tuple-element.44.lo_hbm, ...), custom_call_target="tpu_custom_call" | custom-call | tf_op jit(solution)/shard_map/weight_grads/pallas_call | solution.py:1141
  937.4 0.0 copy-done.2
  937.4 0.6 copy.24
  938.0 0.0 copy-done.1
  938.0 0.6 copy.25
  938.6 0.0 copy-done
  938.6 0.6 copy.26
Async XLA Ops:
  888.2 49.2 %copy-start.2 = (f32[2,4,512]{2,1,0:T(4,128)S(1)}, f32[2,4,512]{2,1,0:T(4,128)}, u32[]{:S(2)}) copy-start(f32[2,4,512]{2,1,0:T(4,128)} %get-tuple-element.75) | copy-start | bytes 49156
  888.2 49.8 %copy-start.1 = (f32[2,4,512]{2,1,0:T(4,128)S(1)}, f32[2,4,512]{2,1,0:T(4,128)}, u32[]{:S(2)}) copy-start(f32[2,4,512]{2,1,0:T(4,128)} %get-tuple-element.76) | copy-start | bytes 49156
  888.2 50.4 %copy-start = (f32[2,4,512]{2,1,0:T(4,128)S(1)}, f32[2,4,512]{2,1,0:T(4,128)}, u32[]{:S(2)}) copy-start(f32[2,4,512]{2,1,0:T(4,128)} %get-tuple-element.80) | copy-start | bytes 49156

commit v4 on v3

--- a/solution.py
+++ b/solution.py
@@ -18,7 +18,9 @@
 ROWS = BATCH * CHUNK
 KB = 128
 NX = 8
+AHEAD = 4
 VMEM_LIMIT = 63 * 1024 * 1024
+STEP_LIMIT = 37 * 1024 * 1024
 
 
 def sigm(v):
@@ -77,13 +79,13 @@
     return jnp.concatenate([bias_ref[layer, g:g + _1, :] for g in GATES], axis=_1)
 
 
-def prep_kernel(wrec_hbm, wup_hbm, win_hbm, x_hbm, gy_hbm, hc_ref, bias_ref,
+def prep_kernel(wrec_hbm, wup_hbm, win_hbm, x_hbm, gy_hbm, h_ref, c_ref, bias_ref,
                 wa_hbm, wb_hbm, wat_hbm, wbt_hbm, wup2_hbm, wupt_hbm, pre_hbm, xt_hbm, gyt_hbm, hcb_ref, init_ref,
                 rin, rup, ra, rb, spread, wst, wtst, win, xin, xf, xb, prev, gyin, gyb, ib, initv, hcv,
                 lsem, osem, jsem, ssx, rsx, ssy, rsy, sss, rss, gsem):
     y, m, x, c = place()
     beside, across, skew = flips(m)
-    hl = hc_ref.shape[3]
+    hl = h_ref.shape[_2]
     per = hl // LANES
     stride = 4 * per
     span = KB * stride
@@ -114,14 +116,16 @@
         dst = initv.at[:, slot, :, pl.ds(pl.multiple_of(c * _2 * hl + x * hl, hl), hl)]
         return remote(ib, dst, sss.at[i], rss.at[i], dev(dest_y, dest_m))
 
-    def state_send():
-        return remote(hc_ref.at[_1 - x], hcv, sss.at[7], rss.at[7], dev(y, across))
-
-    ib[...] = hc_ref[:, _0].astype(BF16)
+    def state_sends():
+        return [remote(ref.at[_1 - x], hcv.at[i], sss.at[7 + i], rss.at[7 + i], dev(y, across))
+                for i, ref in enumerate((h_ref, c_ref))]
+
+    ib[...] = h_ref[...].astype(BF16)
     initv[:, _0, :, pl.ds(pl.multiple_of(c * _2 * hl + x * hl, hl), hl)] = ib[...]
     for i, (oy, om) in enumerate(everyone(y, m)):
         small(i, oy, om).start()
-    state_send().start()
+    for cp in state_sends():
+        cp.start()
     for i in range(NX):
         xsend(i).start()
 
@@ -238,7 +242,8 @@
 
     for i, (oy, om) in enumerate(everyone(y, m)):
         small(i, oy, om).wait()
-    state_send().wait()
+    for cp in state_sends():
+        cp.wait()
     hcb_ref[...] = hcv[...]
     init_ref[...] = initv[...]
 
@@ -263,9 +268,9 @@
     local(prev, pre_hbm, osem.at[_2]).wait()
 
 
-def fwd_kernel(wa_hbm, wb_hbm, wup_hbm, pre_hbm, xt_hbm, hc_ref, hcb_ref, bias_ref,
-               act_hbm, cell_hbm, lown_hbm, loth_hbm, town_hbm, toth_hbm, xoth_hbm, last_ref, fin_ref,
-               w, wup, prea, preb, actv, cellv, histv, hbuf, hch, cst, hs, hr,
+def fwd_kernel(wa_hbm, wb_hbm, wup_hbm, pre_hbm, xt_hbm, wta_hbm, wtb_hbm, h_ref, c_ref, hcb_ref, bias_ref,
+               actv, cellv, wt, lown_hbm, town_hbm, far_hbm, xoth_hbm, last_ref, fin_ref,
+               w, wup, prea, preb, histv, hbuf, hch, cst, hs, hr,
                lsem, psem, osem, xs, xr, hss, hrs, ps, prs, csem, fsem):
     y, m, x, c = place()
     beside, across, skew = flips(m)
@@ -287,6 +292,14 @@
     for cp in loads:
         cp.start()
 
+    def next_loads():
+        out = []
+        for pos, shard in enumerate((beside, skew, m, across)):
+            for row, src in enumerate((wta_hbm, wtb_hbm)):
+                out.append(local(src.at[:, aligned(shard, hl)], wt.at[pl.ds(row * wide, wide), pl.ds(pos * hl, hl)],
+                                 lsem.at[len(out)]))
+        return out
+
     def pre_load(k):
         rows = pl.ds(k * PAIRS, PAIRS)
         return local(pre_hbm.at[rows], prea.at[rows], psem.at[k])
@@ -320,20 +333,22 @@
         def start(i, _):
             pre_send(i).start()
             return _0
-        lax.fori_loop(_0, npair, start, _0)
+        lax.fori_loop(_0, AHEAD * PAIRS, start, _0)
 
     x_send().start()
 
     def low_send(k, i):
         oy, om = others[i]
-        if i < 3:
-            return remote(histv.at[k], hbuf.at[k, :, own_cols], hss.at[i], hrs.at[k, c], dev(oy, om))
-        return remote(histv.at[k], loth_hbm.at[aligned(k, ROWS), own_cols], hss.at[i], csem.at[_0], dev(oy, om))
+        return remote(histv.at[k], hbuf.at[k, :, own_cols], hss.at[i], hrs.at[k, c], dev(oy, om))
 
     def top_send(k, i):
         oy, om = others[i]
-        dst, sem = (town_hbm, csem.at[_1]) if i < 3 else (toth_hbm, csem.at[_2])
-        return remote(histv.at[k], dst.at[aligned(k, ROWS), own_cols], hss.at[i], sem, dev(oy, om))
+        return remote(histv.at[k], town_hbm.at[aligned(k, ROWS), own_cols], hss.at[i], csem.at[_1], dev(oy, om))
+
+    def far_send(k, dx, dc):
+        om = _2 * lax.rem(x + dx, _2) + lax.rem(c + dc, _2)
+        return remote(histv.at[k], far_hbm.at[x, aligned(k, ROWS), own_cols], hss.at[3 + _2 * dx + dc],
+                      csem.at[_2 * x], dev(_1 - y, om))
 
     def hrecv(k, core):
         cols = pl.ds(pl.multiple_of(core * half, half), half)
@@ -342,7 +357,7 @@
     def own_top(k):
         return local(histv.at[k], town_hbm.at[aligned(k, ROWS), own_cols], osem.at[3])
 
-    init = [jnp.where(x == _0, hc_ref[_0], hc_ref[_1]), hcb_ref[...]]
+    init = [[jnp.where(x == _0, ref[_0], ref[_1]) for ref in (h_ref, c_ref)], hcb_ref]
     for s in BOTH:
         units = part(s, hl)
         hs[_0, s] = init[s][_0].astype(BF16)
@@ -387,42 +402,52 @@
         swap(_1 - j, _0).start()
         swap(_1 - j, _1).start()
 
+    def again(make, k, fresh):
+        @pl.when(fresh)
+        def _():
+            make(k - _1).wait_send()
+        make(k).start()
+
+    def feed(k, p):
+        @pl.when((x == _1) & (k + AHEAD < nch))
+        def _():
+            pre_send((k + AHEAD) * PAIRS + p).start()
+
+    def first_turn(k, j):
+        q = k - _1
+        if j == _1:
+            feed(k, _0)
+
+        if j == _0:
+            @pl.when((x == _0) & (q >= _0))
+            def _():
+                for i in (_1, _2):
+                    again(lambda v: low_send(v, i), q, q >= _1)
+
+        @pl.when((x == _1) & (q >= _0))
+        def _():
+            again(lambda v: top_send(v, j), q, q >= _1)
+
+    def turn(k, p, j):
+        q = k - _1
+        if j == _1:
+            feed(k, p)
+
+        @pl.when((x == _0) & (p == _1) & (q >= _0))
+        def _():
+            up_send(q, _2 + j).start()
+
+        if j == _0:
+            @pl.when((x == _1) & (p == _1) & (q >= _0))
+            def _():
+                again(lambda v: top_send(v, _2), q, q >= _1)
+
+        @pl.when((p >= _2) & (q >= _0))
+        def _():
+            again(lambda v: far_send(v, p - _2, j), q, q >= _1)
+
     def up_product(k, at):
         prea[pl.ds(at, PAIRS)] = (mm(hbuf[k], wup[...]) + gate_row(bias_ref, _1)).reshape(PAIRS, 8, wide)
-
-    def again(make, k, fresh):
-        @pl.when(fresh)
-        def _():
-            make(k - _1).wait_send()
-        make(k).start()
-
-    def low_copy(i):
-        return lambda k: low_send(k, i)
-
-    def up_copy(p):
-        return lambda k: up_send(k, p)
-
-    low_turns = ((_1,), (_2,), ('up', _1), ('up', _2), ('up', 3), (3,), (4,), (5, 6))
-
-    def turn(k, e):
-        q = k - _1
-
-        @pl.when((x == _0) & (q >= _0))
-        def _():
-            if low_turns[e][_0] == 'up':
-                up_copy(low_turns[e][_1])(q).start()
-            else:
-                for i in low_turns[e]:
-                    again(low_copy(i), q, q >= _1)
-
-        if e < 7:
-            @pl.when((x == _1) & (q >= _0))
-            def _():
-                again(lambda kk: top_send(kk, e), q, q >= _1)
-
-    def act_out(k):
-        rows = pl.ds(k * PAIRS, PAIRS)
-        return local(actv.at[rows], act_hbm.at[rows], osem.at[_0])
 
     def slot_body(s, _):
         k = s - x
@@ -442,7 +467,7 @@
             @pl.when(final)
             def _():
                 for i in (_1, _2):
-                    again(low_copy(i), nch - _1, True)
+                    again(lambda v: low_send(v, i), nch - _1, True)
                 for p in range(PAIRS):
                     up_send(nch - _2, p).wait_send()
             up_product(q, x * k * PAIRS + (_1 - x) * npair)
@@ -451,8 +476,9 @@
             def _():
                 for p in range(PAIRS):
                     up_send(nch - _1, p).start()
-                for i in range(3, 7):
-                    again(low_copy(i), nch - _1, True)
+                for dx in BOTH:
+                    for dc in BOTH:
+                        again(lambda v: far_send(v, dx, dc), nch - _1, True)
 
         @pl.when(live)
         def _():
@@ -460,8 +486,13 @@
             def _():
                 pre_load(k).wait()
 
+            @pl.when(k == nch - _1)
+            def _():
+                for cp in next_loads():
+                    cp.start()
+
             up_send(k, _0).wait_recv()
-            step(k, _0, _0, lambda: turn(k, _0))
+            step(k, _0, _0, lambda: first_turn(k, _0))
 
             @pl.when((x == _0) & (k >= _1))
             def _():
@@ -473,31 +504,24 @@
                         up_send(k - _2, p).wait_send()
                 up_product(k - _1, npair)
                 up_send(k - _1, _0).start()
-
-            step(k, _0, _1, lambda: turn(k, _1))
+                up_send(k - _1, _1).start()
+
+            step(k, _0, _1, lambda: first_turn(k, _1))
 
             def pair_body(p, _):
-                def turn_of(j):
-                    for pp in range(_1, PAIRS):
-                        @pl.when(p == pp)
-                        def _():
-                            turn(k, _2 * pp + j)
-
                 up_send(k, p).wait_recv()
-                step(k, p, _0, lambda: turn_of(_0))
-                step(k, p, _1, lambda: turn_of(_1))
+                step(k, p, _0, lambda: turn(k, p, _0))
+                step(k, p, _1, lambda: turn(k, p, _1))
                 return _0
 
             lax.fori_loop(_1, PAIRS, pair_body, _0)
-            act_out(k).start()
-
             @pl.when(x == _0)
             def _():
                 block = hch[...].reshape(ROWS, half).astype(BF16)
                 histv[k] = block
                 hbuf[k, :, own_cols] = block
 
-                again(low_copy(_0), k, k >= _1)
+                again(lambda v: low_send(v, _0), k, k >= _1)
 
             @pl.when(x == _1)
             def _():
@@ -509,7 +533,6 @@
         return _0
 
     lax.fori_loop(_0, nch + _1, slot_body, _0)
-    local(cellv, cell_hbm, osem.at[_2]).start()
     swap(_0, _0).wait()
     swap(_0, _1).wait()
     last_ref[...] = histv[nch - _1]
@@ -521,8 +544,11 @@
 
     @pl.when(x == _0)
     def _():
-        for i in range(7):
+        for i in range(3):
             low_send(nch - _1, i).wait_send()
+        for dx in BOTH:
+            for dc in BOTH:
+                far_send(nch - _1, dx, dc).wait_send()
         for p in range(PAIRS):
             up_send(nch - _1, p).wait_send()
         whole = town_hbm.at[sent, :]
@@ -530,8 +556,11 @@
 
     @pl.when(x == _1)
     def _():
-        for i in range(7):
+        for i in range(3):
             top_send(nch - _2, i).wait_send()
+        for dx in BOTH:
+            for dc in BOTH:
+                far_send(nch - _2, dx, dc).wait_send()
         local(pre_hbm, pre_hbm, fsem.at[_0]).wait()
         part = town_hbm.at[sent, pl.ds(_0, half)]
         local(part, part, csem.at[_1]).wait()
@@ -546,19 +575,19 @@
         return _0
 
     lax.fori_loop(_0, nch, low_start, _0)
-    local(loth_hbm, loth_hbm, csem.at[_0]).wait()
-    far = toth_hbm.at[sent, :]
+    local(far_hbm.at[_0], far_hbm.at[_0], csem.at[_0]).wait()
+    far = far_hbm.at[_1, sent, :]
     local(far, far, csem.at[_2]).wait()
     x_send().wait()
     local(lown_hbm, lown_hbm, osem.at[_1]).wait()
-    local(cellv, cell_hbm, osem.at[_2]).wait()
-    local(actv, act_hbm, osem.at[_0]).wait()
-
-
-def bwd_kernel(wta_hbm, wtb_hbm, wupt_hbm, act_hbm, cell_hbm, gy_hbm, last_ref, fin_ref,
+    for cp in next_loads():
+        cp.wait()
+
+
+def bwd_kernel(wupt_hbm, gy_hbm, actv, cellv, wt, last_ref, fin_ref,
                dg_hbm, tlo_hbm, tlf_hbm, bias_ref, hfin_ref, cfin_ref,
-               wt, wupt, actv, cellv, dout, gyv, dgv, dgr, dgch, dgs, dct, bacc, own, snd, rcv, pin, pout, bsnd, brcv, finr,
-               lsem, asem, osem, xs, xr, gs, grs, ps, prs, csem, bsem, tsem):
+               wupt, dout, gyv, dgv, dgr, dgch, dgs, dct, bacc, own, snd, rcv, pin, pout, bsnd, brcv, finr,
+               lsem, osem, xs, xr, gs, grs, ps, prs, csem, bsem, tsem):
     y, m, x, c = place()
     beside, across, skew = flips(m)
     nch = dgv.shape[_0]
@@ -568,33 +597,14 @@
     hp = PAIRS // _2
     hr = ROWS // _2
 
-    first_loads = [local(cell_hbm, cellv, lsem.at[12])]
-    loads = []
-    for pos, shard in enumerate((beside, skew, m, across)):
-        for row, src in enumerate((wta_hbm, wtb_hbm)):
-            loads.append(local(src.at[:, aligned(shard, hl)], wt.at[pl.ds(row * wide, wide), pl.ds(pos * hl, hl)],
-                               lsem.at[len(loads)]))
-    up_loads = [local(wupt_hbm.at[:, aligned(shard, hl)], wupt.at[:, pl.ds(pos * hl, hl)], lsem.at[8 + pos])
+    up_loads = [local(wupt_hbm.at[:, aligned(shard, hl)], wupt.at[:, pl.ds(pos * hl, hl)], lsem.at[pos])
                 for pos, shard in enumerate((_1 - c, 3 - c, c, _2 + c))]
 
-    def act_in(k):
-        rows = pl.ds(k * PAIRS, PAIRS)
-        return local(act_hbm.at[rows], actv.at[rows], asem.at[k])
-
     @pl.when(x == _1)
     def _():
-        local(gy_hbm, gyv, lsem.at[13]).start()
-    for cp in first_loads:
+        local(gy_hbm, gyv, lsem.at[4]).start()
+    for cp in up_loads:
         cp.start()
-    act_in(nch - _1).start()
-    for cp in loads + up_loads:
-        cp.start()
-
-    def start_act(i, _):
-        act_in(nch - _2 - i).start()
-        return _0
-
-    lax.fori_loop(_0, nch - _1, start_act, _0)
     entry_barrier(y, m)
 
     own_cols = pl.ds(pl.multiple_of(c * half, half), half)
@@ -636,12 +646,11 @@
         return remote(dgv.at[k, pl.ds(h * hr, hr), part_b], dg_hbm.at[_0, _0, half_rows(k, h), :],
                       gs.at[_0, h], csem.at[_2], dev(y, across))
 
-    def wider(k, h, top):
-        rows = pl.ds(h * hr, hr)
-        layer = _1 if top else _0
-        dst = dg_hbm.at[layer, _1, half_rows(k, h), :]
-        return (remote(dgv.at[k, rows, part_a], dst, gs.at[_1, h], csem.at[_0], dev(_1 - y, m)),
-                remote(dgv.at[k, rows, part_b], dst, gs.at[_2, h], csem.at[_1], dev(_1 - y, across)))
+    def wider(k, h, i):
+        rows = pl.ds(pl.multiple_of(h * hr, hr), hr)
+        dst = dg_hbm.at[x, _1, pl.ds(pl.multiple_of(k * ROWS + h * hr, hr), hr), :]
+        src, other = ((part_a, m), (part_b, across))[i]
+        return remote(dgv.at[k, rows, src], dst, gs.at[_1 + i, h], csem.at[i], dev(_1 - y, other))
 
     def keep(k, h, top):
         return local(dgv.at[k, pl.ds(h * hr, hr), part_a], dg_hbm.at[_1 if top else _0, _0, half_rows(k, h), :], osem.at[_0])
@@ -664,7 +673,7 @@
 
     @pl.when(x == _1)
     def _():
-        local(gy_hbm, gyv, lsem.at[13]).wait()
+        local(gy_hbm, gyv, lsem.at[4]).wait()
         for s in BOTH:
             dout[:, :, part(s, hl)] = gyv[s].astype(F32).reshape(nch * PAIRS, 8, hl)
 
@@ -672,8 +681,6 @@
     def _():
         for cp in up_loads:
             cp.wait()
-    for cp in first_loads:
-        cp.wait()
 
     def point(k, p, j, inner):
         pair = k * PAIRS + p
@@ -714,32 +721,30 @@
     def near_copy(h, top):
         return lambda k: near(k, h, top)
 
-    def wide_copy(h, top, i):
-        return lambda k: wider(k, h, top)[i]
-
-    def turn(k, e):
+    def first_turn(k, e):
         late = k < nch - _1
 
-        if e < 3:
+        if e == _0:
             @pl.when((x == _0) & late)
             def _():
-                again((near_copy(_0, False), wide_copy(_0, False, _0), wide_copy(_0, False, _1))[e], k + _1)
-        if e in (4, 5, 6):
-            @pl.when(x == _0)
-            def _():
-                again((near_copy(_1, False), wide_copy(_1, False, _0), wide_copy(_1, False, _1))[e - 4], k)
-        if e < _2:
-            @pl.when((x == _1) & late)
-            def _():
-                up_sends(k + _1, e)[_1].start()
-        if e in (_2, 3):
-            @pl.when((x == _1) & late)
-            def _():
-                again(wide_copy(_0, True, e - _2), k + _1)
-        if e in (5, 6):
-            @pl.when(x == _1)
-            def _():
-                again(wide_copy(_1, True, e - 5), k)
+                again(near_copy(_0, False), k + _1)
+
+        @pl.when((x == _1) & late)
+        def _():
+            up_sends(k + _1, e)[_1].start()
+
+    def turn(k, p, j):
+        back = p - _1
+        q = k + back
+
+        @pl.when((p >= _1) & (q < nch))
+        def _():
+            again(lambda v: wider(v, _1 - back, _1 - j), q)
+
+        if j == _1:
+            @pl.when((p == _0) & (x == _0))
+            def _():
+                again(near_copy(_1, False), k)
 
     def emit(k, h):
         dgv[k, part(h, hr), :] = dgch[part(h, hp)].reshape(hr, _2 * wide).astype(BF16)
@@ -786,13 +791,9 @@
 
         @pl.when(live)
         def _():
-            act_in(k).wait()
-
             @pl.when(first)
             def _():
                 point(k, PAIRS - _1, _1, False)
-                for cp in loads:
-                    cp.wait()
 
                 @pl.when(x == _1)
                 def _():
@@ -801,8 +802,8 @@
 
             @pl.when(k < nch - _1)
             def _():
-                step(k, PAIRS - _1, _1, lambda: turn(k, _0))
-            step(k, PAIRS - _1, _0, lambda: turn(k, _1))
+                step(k, PAIRS - _1, _1, lambda: first_turn(k, _0))
+            step(k, PAIRS - _1, _0, lambda: first_turn(k, _1))
 
             def pair_body(i, _):
                 p = PAIRS - _2 - i
@@ -811,14 +812,8 @@
                 def _():
                     take(k, _0)
 
-                def turn_of(j):
-                    for pp in range(PAIRS - _1):
-                        @pl.when(p == pp)
-                        def _():
-                            turn(k, _2 * (PAIRS - _1 - pp) + _1 - j)
-
-                step(k, p, _1, lambda: turn_of(_1))
-                step(k, p, _0, lambda: turn_of(_0))
+                step(k, p, _1, lambda: turn(k, p, _1))
+                step(k, p, _0, lambda: turn(k, p, _0))
 
                 @pl.when(p == hp)
                 def _():
@@ -846,15 +841,13 @@
     @pl.when(x == _0)
     def _():
         again(near_copy(_0, False), _0)
-        for i in BOTH:
-            again(wide_copy(_0, False, i), _0)
 
     @pl.when(x == _1)
     def _():
         for pos in BOTH:
             up_sends(_0, pos)[_1].start()
-        for i in BOTH:
-            again(wide_copy(_0, True, i), _0)
+    for i in BOTH:
+        again(lambda v: wider(v, _0, i), _0)
 
     bsnd[_0] = bacc[:, _0:wide]
     bsnd[_1] = bacc[:, wide:]
@@ -877,8 +870,6 @@
             cp.wait_send()
         for h in BOTH:
             near(_0, h, False).wait_send()
-            for cp in wider(_0, h, False):
-                cp.wait_send()
         local(quarter, quarter, osem.at[_1]).wait()
         local(tlo_hbm, tlo_hbm, tsem.at[9]).wait()
 
@@ -889,14 +880,15 @@
                 cp.wait_send()
         for h in BOTH:
             near(_0, h, True).wait_send()
-            for cp in wider(_0, h, True):
-                cp.wait_send()
         local(quarter, quarter, csem.at[_2]).wait()
         for cp in last_sends():
             cp.wait_send()
         local(last_ref, last_ref, tsem.at[9]).wait()
         last_keep().wait()
 
+    for h in BOTH:
+        for i in BOTH:
+            wider(_0, h, i).wait_send()
     local(tlf_hbm, tlf_hbm, tsem.at[10]).wait()
     local(quarter, quarter, csem.at[_0]).wait()
     local(quarter, quarter, csem.at[_1]).wait()
@@ -912,8 +904,8 @@
         bias_ref[_1, g:g + _1, :] = top[:, part(g, hl)]
 
 
-def grad_kernel(xo_hbm, xf_hbm, lo_hbm, lf_hbm, to_hbm, tf_hbm, tlo_hbm, tlf_hbm, init_ref, dg_hbm,
-                dwin_hbm, dwup_hbm, dwrec_hbm, y_ref,
+def grad_kernel(xo_hbm, xf_hbm, lo_hbm, to_hbm, far_hbm, tlo_hbm, tlf_hbm, init_ref, hs_ref, cs_ref, bs_ref, dg_hbm,
+                dwin_hbm, dwup_hbm, dwrec_hbm, y_ref, hfin_ref, cfin_ref, bias_ref,
                 lhs, grads, htop, shf, yf, lhst0, lhst1, pieces0, pieces1, lsem, osem):
     hidden = htop.shape[_1]
     srows = lo_hbm.shape[_0]
@@ -931,9 +923,9 @@
     hi = pl.ds(srows, srows)
     body_rows = pl.ds(_0, srows - ROWS)
     srcs = ((xo_hbm, lhs.at[_0, lo, :]), (xf_hbm, lhs.at[_0, hi, :]), (dg_hbm.at[_0, _0], grads.at[_0, lo, :]), (dg_hbm.at[_0, _1], grads.at[_0, hi, :]),
-            (lo_hbm, lhs.at[_1, lo, :]), (lf_hbm, lhs.at[_1, hi, :]), (dg_hbm.at[_1, _0], grads.at[_1, lo, :]), (dg_hbm.at[_1, _1], grads.at[_1, hi, :]),
+            (lo_hbm, lhs.at[_1, lo, :]), (far_hbm.at[_0], lhs.at[_1, hi, :]), (dg_hbm.at[_1, _0], grads.at[_1, lo, :]), (dg_hbm.at[_1, _1], grads.at[_1, hi, :]),
             (to_hbm.at[body_rows, :], htop.at[body_rows, :]),
-            (tf_hbm.at[body_rows, :], htop.at[pl.ds(srows, srows - ROWS), :]),
+            (far_hbm.at[_1, body_rows, :], htop.at[pl.ds(srows, srows - ROWS), :]),
             (tlo_hbm, htop.at[pl.ds(srows - ROWS, ROWS), :]), (tlf_hbm, htop.at[pl.ds(_2 * srows - ROWS, ROWS), :]))
     loads = [local(a, b, lsem.at[i]) for i, (a, b) in enumerate(srcs)]
     for cp in loads:
@@ -978,6 +970,8 @@
         lhst[slot][...] = lhs[n // nblk, :, aligned(lax.rem(n, nblk), kb)].T
 
     total = 4 * nblk
+    for ref, dst in ((hs_ref, hfin_ref), (cs_ref, cfin_ref), (bs_ref, bias_ref)):
+        dst[...] = ref[...]
     for cp in loads[_0:4]:
         cp.wait()
     prepare(_0, _0)
@@ -1034,11 +1028,11 @@
 DMA = pltpu.SemaphoreType.DMA
 
 
-def comm_params(i):
-    return pltpu.CompilerParams(collective_id=i, has_side_effects=True, vmem_limit_bytes=VMEM_LIMIT)
-
-
-def run_prep(wrec, wup, win, x, gy, hc, bias):
+def comm_params(i, limit=VMEM_LIMIT):
+    return pltpu.CompilerParams(collective_id=i, has_side_effects=True, vmem_limit_bytes=limit)
+
+
+def run_prep(wrec, wup, win, x, gy, h, c, bias):
     batch, seq, width = x.shape
     hl = gy.shape[_2]
     wide = 4 * hl
@@ -1054,7 +1048,7 @@
         name='lstm_prepare',
         out_shape=(square,) * 6 + (sds((rows // 8, 8, wide), F32), sds((rows, width), BF16), sds((_2, rows, hl), BF16),
                                    sds((_2, 4, hl), F32), sds((_2, _2, 4, hidden), BF16)),
-        in_specs=[any_spec()] * 5 + [vmem_spec()] * _2,
+        in_specs=[any_spec()] * 5 + [vmem_spec()] * 3,
         out_specs=(any_spec(),) * 9 + (vmem_spec(),) * _2,
         scratch_shapes=[
             vm((raw, LANES), BF16), vm((raw, LANES), BF16), vm((raw, LANES), BF16), vm((raw, LANES), BF16),
@@ -1062,13 +1056,13 @@
             vm(x.shape, BF16), vm((4, rows, LANES), F32), vm((rows, width), BF16), vm((rows // 8, 8, wide), F32),
             vm(gy.shape, BF16), vm((rows, hl), BF16), vm((_2, 4, hl), BF16),
             vm((_2, _2, 4, hidden), BF16), vm((_2, 4, hl), F32),
-            DMA((5,)), DMA((3,)), DMA((6, _2)), DMA((NX,)), DMA((NX,)), DMA((NX,)), DMA((NX,)), DMA((8,)), DMA((8,)), DMA((_2,)),
+            DMA((5,)), DMA((3,)), DMA((6, _2)), DMA((NX,)), DMA((NX,)), DMA((NX,)), DMA((NX,)), DMA((9,)), DMA((9,)), DMA((_2,)),
         ],
         compiler_params=comm_params(_0),
-    )(wrec, wup, win, x, gy, hc, bias)
-
-
-def run_fwd(wa, wb, wup, pre, xt, hc, hcb, bias):
+    )(wrec, wup, win, x, gy, h, c, bias)
+
+
+def run_fwd(wa, wb, wup, pre, xt, wta, wtb, h, c, hcb, bias):
     hidden, wide = wa.shape
     hl = wide // 4
     half = _2 * hl
@@ -1080,26 +1074,26 @@
     return pl.pallas_call(
         fwd_kernel,
         name='lstm_forward',
-        out_shape=(sds((npair, 8, _2 * wide), F32), sds((npair + _1, 8, half), F32), hist, hist, hist, hist,
+        out_shape=(vm((npair, 8, _2 * wide), F32), vm((npair + _1, 8, half), F32), vm((_2 * wide, hidden), BF16),
+                   hist, hist, sds((_2, rows, hidden), BF16),
                    sds(xt.shape, BF16), sds((ROWS, half), BF16), sds((_2, _2, 4, hl), F32)),
-        in_specs=[any_spec()] * 5 + [vmem_spec()] * 3,
-        out_specs=(any_spec(),) * 7 + (vmem_spec(),) * _2,
+        in_specs=[any_spec()] * 7 + [vmem_spec()] * 4,
+        out_specs=(vmem_spec(),) * 3 + (any_spec(),) * 4 + (vmem_spec(),) * _2,
         scratch_shapes=[
             vm((hidden, _2 * wide), BF16), vm((hidden, wide), BF16),
             vm((npair + PAIRS, 8, wide), F32), vm((npair, 8, wide), F32),
-            vm((npair, 8, _2 * wide), F32), vm((npair + _1, 8, half), F32),
             vm((nch, ROWS, half), BF16), vm((nch, ROWS, hidden), BF16),
             vm((PAIRS, 8, half), F32), vm((4, half), F32),
             vm((_2, _2, 4, hl), BF16), vm((_2, _2, 4, hl), BF16),
             DMA((12,)), DMA((nch,)), DMA((4,)), DMA((_2, _2)), DMA((_2, _2)), DMA((7,)), DMA((nch, _2)),
             DMA((PAIRS,)), DMA((npair,)), DMA((3,)), DMA((3,)),
         ],
-        compiler_params=comm_params(_1),
-    )(wa, wb, wup, pre, xt, hc, hcb, bias)
-
-
-def run_bwd(wta, wtb, wupt, act, cell, gy, last, fin):
-    wide, hidden = wta.shape
+        compiler_params=comm_params(_1, STEP_LIMIT),
+    )(wa, wb, wup, pre, xt, wta, wtb, h, c, hcb, bias)
+
+
+def run_bwd(wupt, gy, act, cell, wt, last, fin):
+    wide, hidden = wupt.shape
     hl = wide // 4
     half = _2 * hl
     npair = act.shape[_0]
@@ -1111,26 +1105,24 @@
         bwd_kernel,
         name='lstm_backward',
         out_shape=(sds((_2, _2, rows, wide), BF16), sds((ROWS, hidden), BF16), sds((ROWS, hidden), BF16), state, state, state),
-        in_specs=[any_spec()] * 6 + [vmem_spec()] * _2,
+        in_specs=[any_spec()] * _2 + [vmem_spec()] * 5,
         out_specs=(any_spec(),) * 3 + (vmem_spec(),) * 3,
         scratch_shapes=[
-            vm((_2 * wide, hidden), BF16), vm((wide, hidden), BF16),
-            vm((npair, 8, _2 * wide), F32), vm((npair + _1, 8, half), F32),
-            vm((npair, 8, half), F32), vm((_2, rows, hl), BF16),
+            vm((wide, hidden), BF16), vm((npair, 8, half), F32), vm((_2, rows, hl), BF16),
             vm((nch, ROWS, _2 * wide), BF16), vm((nch, ROWS, wide), BF16),
             vm((PAIRS, 8, _2 * wide), F32), vm((4, _2 * wide), BF16),
             vm((4, half), F32), vm((8, _2 * wide), F32),
             vm((4, half), F32), vm((_2, 4, half), F32), vm((_2, 4, half), F32),
             vm((3, nch, PAIRS, 8, half), F32), vm((_2, PAIRS, 8, half), F32),
             vm((_2, 8, wide), F32), vm((3, 8, wide), F32), vm((_2, 4, hl), F32),
-            DMA((14,)), DMA((nch,)), DMA((_2,)), DMA((_2,)), DMA((_2,)), DMA((3, _2)), DMA((nch, _2)), DMA((_2, _2)), DMA((3, nch, _2)),
+            DMA((5,)), DMA((_2,)), DMA((_2,)), DMA((_2,)), DMA((3, _2)), DMA((nch, _2)), DMA((_2, _2)), DMA((3, nch, _2)),
             DMA((3,)), DMA((6,)), DMA((12,)),
         ],
-        compiler_params=comm_params(_2),
-    )(wta, wtb, wupt, act, cell, gy, last, fin)
-
-
-def run_grads(xo, xf, lo, lf, to, tf, tlo, tlf, init, dg):
+        compiler_params=comm_params(_2, STEP_LIMIT),
+    )(wupt, gy, act, cell, wt, last, fin)
+
+
+def run_grads(xo, xf, lo, to, far, tlo, tlf, init, small, dg):
     srows, hidden = lo.shape
     rows = _2 * srows
     wide = dg.shape[3]
@@ -1142,14 +1134,14 @@
         grad_kernel,
         name='weight_grads',
         out_shape=(sds((hidden,) + tile, F32), sds((hidden,) + tile, F32), sds((_2 * hidden,) + tile, F32),
-                   sds((BATCH, srows // BATCH, hl), BF16)),
-        in_specs=[any_spec()] * 8 + [vmem_spec(), any_spec()],
-        out_specs=(any_spec(),) * 3 + (vmem_spec(),),
+                   sds((BATCH, srows // BATCH, hl), BF16)) + (sds((_2, 4, hl), F32),) * 3,
+        in_specs=[any_spec()] * 7 + [vmem_spec()] * 4 + [any_spec()],
+        out_specs=(any_spec(),) * 3 + (vmem_spec(),) * 4,
         scratch_shapes=[vm((4, rows, hidden), BF16), vm((_2, rows, wide), BF16), vm((rows, hidden), BF16),
                         vm((rows, kb), F32), vm((hl // LANES, srows, LANES), F32), vm((kb, rows), BF16), vm((kb, rows), BF16),
                         vm((wide // LANES, kb, LANES), F32), vm((wide // LANES, kb, LANES), F32), DMA((12,)), DMA((_2,))],
         compiler_params=pltpu.CompilerParams(vmem_limit_bytes=VMEM_LIMIT),
-    )(xo, xf, lo, lf, to, tf, tlo, tlf, init, dg)
+    )(xo, xf, lo, to, far, tlo, tlf, init, *small, dg)
 
 
 def to_raw(w):
@@ -1175,14 +1167,14 @@
 
     def local_program(x_seq, gy_seq, h_init, c_init, w_in, w_up, w_rec, gate_bias):
         hl = w_in.shape[_2]
-        hc = jnp.stack([h_init, c_init], axis=_1)
         wa, wb, wat, wbt, wup, wupt, pre, xt, gyt, hcb, init = run_prep(
-            to_raw(w_rec), to_raw(w_up), to_raw(w_in), x_seq, gy_seq, hc, gate_bias)
-        act, cell, low_own, low_far, top_own, top_far, x_far, last, fin = run_fwd(
-            wa, wb, wup, pre, xt, hc, hcb, gate_bias)
-        dg, last_own, last_far, bias, h_last, c_last = run_bwd(wat, wbt, wupt, act, cell, gyt, last, fin)
-        dw_in, dw_up, dw_rec, y_out = run_grads(
-            xt, x_far, low_own, low_far, top_own, top_far, last_own, last_far, init, dg)
+            to_raw(w_rec), to_raw(w_up), to_raw(w_in), x_seq, gy_seq, h_init, c_init, gate_bias)
+        act, cell, wt, low_own, top_own, far, x_far, last, fin = run_fwd(
+            wa, wb, wup, pre, xt, wat, wbt, h_init, c_init, hcb, gate_bias)
+        act, cell, wt = (pltpu.with_memory_space_constraint(v, pltpu.VMEM) for v in (act, cell, wt))
+        dg, last_own, last_far, bias, h_last, c_last = run_bwd(wupt, gyt, act, cell, wt, last, fin)
+        dw_in, dw_up, dw_rec, y_out, h_last, c_last, bias = run_grads(
+            xt, x_far, low_own, top_own, far, last_own, last_far, init, (h_last, c_last, bias), dg)
         return (y_out, h_last, c_last, from_raw(dw_in, (), hl), from_raw(dw_up, (_1,), hl),
                 from_raw(dw_rec, (_2,), hl), bias)
 

time: 940 us -> 920 us (0.979)
  Pallas kernels: 935 us -> 919 us
where the time goes in v4:
time: 920 us
  Pallas kernels  919 us (100%)
    pallas_call x1, Pallas kernels, run_fwd(): pl.pallas_call(fwd_kernel, name='lstm_forward', out_shape=(vm((npair, 8,...  381 us
    pallas_call x1, Pallas kernels, run_bwd(): pl.pallas_call(bwd_kernel, name='lstm_backward', out_shape=(sds((_2, _2,...  377 us
    pallas_call x1, Pallas kernels, run_prep(): pl.pallas_call(prep_kernel, name='lstm_prepare', out_shape=(square,) * 6...  112 us
    pallas_call x1, Pallas kernels, run_grads(): pl.pallas_call(grad_kernel, name='weight_grads', out_shape=(sds((hidden,)...  49.2 us

profile of v4, /device:TPU:0, one launch (start us, length us, event | category | flops | bytes accessed | tf_op | source)
XLA Modules:
  0.0 919.7 jit_solution(17105241354508959528)
XLA Ops:
  0.6 112.4 %lstm_prepare.1 = (bf16[2048,2048]{1,0:T(8,128)(2,1)}, bf16[2048,2048]{1,0:T(8,128)(2,1)}, bf16[2048,2048]{1,0:T(8,128)(2,1)}, bf16[2048,2048]{1,0:T(8,128)(2,1)...) custom-call(bf16[65536,128]{1,0:T(8,128)(2,1)} %bitcast.30, ...), custom_call_target="tpu_custom_call" | custom-call | tf_op jit(solution)/shard_map/lstm_prepare/pallas_call | solution.py:1046
  113.0 380.7 %lstm_forward.1 = (f32[64,8,4096]{2,1,0:T(8,128)S(1)}, f32[65,8,1024]{2,1,0:T(8,128)S(1)}, bf16[4096,2048]{1,0:T(8,128)(2,1)S(1)}, bf16[512,2048]{1,0:T(8,128)(2...) custom-call(bf16[2048,2048]{1,0:T(8,128)(2,1)} %get-tuple-element.41, ...), custom_call_target="tpu_custom_call" | custom-call | tf_op jit(solution)/shard_map/lstm_forward/pallas_call | solution.py:1074
  493.7 376.6 %lstm_backward.1 = (bf16[2,2,512,2048]{3,2,1,0:T(8,128)(2,1)}, bf16[32,2048]{1,0:T(8,128)(2,1)}, bf16[32,2048]{1,0:T(8,128)(2,1)}, f32[2,4,512]{2,1,0:T(4,128)},...) custom-call(bf16[2048,2048]{1,0:T(8,128)(2,1)} %get-tuple-element.52.wupt_hbm, ...), custom_call_target="tpu_custom_call" | custom-call | tf_op jit(solution)/shard_map/lstm_backward/pallas_call | solution.py:1104
  870.3 49.2 %weight_grads.1 = (f32[2048,16,128]{2,1,0:T(8,128)}, f32[2048,16,128]{2,1,0:T(8,128)}, f32[4096,16,128]{2,1,0:T(8,128)}, bf16[4,128,512]{2,1,0:T(8,128)(2,1)}, f...) custom-call(bf16[512,2048]{1,0:T(8,128)(2,1)} %get-tuple-element.40.xt_hbm.xo_hbm, ...), custom_call_target="tpu_custom_call" | custom-call | tf_op jit(solution)/shard_map/weight_grads/pallas_call | solution.py:1133
